TPU v7x, 128 devices: a whole 4x4x4 slice. The times are simulated.
128 devices in a mesh: gx: 16 (over z, x), yz: 8 (over y, core).
Axes of the slice: x: 4, y: 4, z: 4, core: 2. Of those that a mesh axis runs over, the one named last changes fastest.
Arguments:
- state: float32 [4, 512, 384, 256], P(None, 'gx', 'yz'), may hold values from -6 to 6
- mean_flow: float32 [512, 384, 256], P('gx', 'yz'), may hold values from 0.2 to 1.2
- face_cell: int32 [24576], P(('gx', 'yz')), may hold values from 0 to 50331647, as said below
- face_normal: float32 [3, 24576], P(None, ('gx', 'yz')), may hold values from -3 to 3
- face_pos: float32 [3, 24576], P(None, ('gx', 'yz')), may hold values from -2 to 2
- observer_pos: float32 [3, 512], replicated, may hold values from 4 to 12
- time_bin: int32 [24576, 512], P(('gx', 'yz')), may hold values from 0 to 63
Outputs:
- state_next: float32 [4, 512, 384, 256], P(None, 'gx', 'yz')
- signal: float32 [512, 64], P(('gx', 'yz'))
Inputs may be any that keep to these rules, and one draw needn't show every extreme that they name: `face_cell`: face j is held by device j // 192 of gx+yz, and its cell, numbered (x 384 + y) * 256 + z, lies in that device's block of grid cells.
All inputs are finite; a program needn't handle non-finite values.
Results may differ from a plain program's by a relative error of at most 0.000084.
Values sent between devices are 32-bit elements; how exact they have to be, the bound alone decides.
A program may use at most 192 MiB of HBM per device.

v0:
```python
import jax
import jax.numpy as jnp
from jax import lax
from jax.sharding import Mesh
from jax.sharding import PartitionSpec as P

BINS = 64
GX = ("gx_0", "gx_1")
YZ = ("yz_0", "yz_1")
GX_YZ = ("gx_0", "gx_1", "yz_0", "yz_1")


time_step = 0.25
four_pi = 4.0 * 3.141592653589793
highest = lax.Precision.HIGHEST


def extended(block, sides, width):
    for axis, dim in sides:
        count = lax.axis_size(axis)
        forward = [(i, i + 1) for i in range(count - 1)]
        backward = [(target, source) for source, target in forward]
        low = lax.ppermute(
            lax.slice_in_dim(block, block.shape[dim] - width, None, axis=dim), axis, forward
        )
        high = lax.ppermute(lax.slice_in_dim(block, 0, width, axis=dim), axis, backward)
        block = jnp.concatenate([low, block, high], axis=dim)
    return block


def sum_in_order(pieces, axes, turns):
    inside = pieces.shape[1:]
    pieces = pieces.reshape(*(lax.axis_size(a) for a in axes), *inside)
    pieces = jnp.moveaxis(pieces, turns, range(len(axes))).reshape(-1, *inside)
    for k in turns:
        pieces = lax.psum_scatter(pieces, axes[k], scatter_dimension=0, tiled=True)
    return pieces[0]


def cut_along(shard, dim, peers):
    shape = shard.shape
    pieces = shard.reshape(*shape[:dim], peers, shape[dim] // peers, *shape[dim + 1 :])
    return jnp.moveaxis(pieces, dim, 0)


def sum_by_axis_2(shard, axes, turns, dim):
    peers = lax.axis_size(axes)
    return sum_in_order(cut_along(shard, dim, peers), axes, turns)


def diagonals(count):
    index = jnp.arange(count)
    third = jnp.full((count,), 1.0 / 3.0, jnp.float32)
    quarter = jnp.float32(0.25)
    lower = jnp.where(index == 1, quarter, third)
    lower = jnp.where(index == count - 2, quarter, lower)
    lower = jnp.where(index == count - 1, jnp.float32(2.0), lower)
    lower = jnp.where(index == 0, jnp.float32(0.0), lower)
    upper = jnp.where(index == 1, quarter, third)
    upper = jnp.where(index == count - 2, quarter, upper)
    upper = jnp.where(index == 0, jnp.float32(2.0), upper)
    upper = jnp.where(index == count - 1, jnp.float32(0.0), upper)
    return (lower, jnp.ones((count,), jnp.float32), upper)


def inverse_of(lower, middle, upper):
    count = middle.shape[0]
    return lax.linalg.tridiagonal_solve(lower, middle, upper, jnp.eye(count, dtype=jnp.float32))


def compact_rhs(field, axis):
    count = field.shape[axis]
    widths = [(2, 2) if dimension == axis else (0, 0) for dimension in range(field.ndim)]
    padded = jnp.pad(field, widths)

    def take(first, last):
        return lax.slice_in_dim(padded, first, last, axis=axis)

    def plane(index):
        return lax.slice_in_dim(field, index, index + 1, axis=axis)

    inner = 7.0 / 9.0 * (take(3, count + 3) - take(1, count + 1)) + 1.0 / 36.0 * (
        take(4, count + 4) - take(0, count)
    )
    first_row = 0.5 * (4.0 * plane(1) + plane(2) - 5.0 * plane(0))
    second_row = 0.75 * (plane(2) - plane(0))
    before_last = 0.75 * (plane(count - 1) - plane(count - 3))
    last_row = 0.5 * (5.0 * plane(count - 1) - 4.0 * plane(count - 2) - plane(count - 3))
    middle_rows = lax.slice_in_dim(inner, 2, count - 2, axis=axis)
    return jnp.concatenate([first_row, second_row, middle_rows, before_last, last_row], axis)


def explicit_y(padded, count):

    def take(shift):
        return lax.slice_in_dim(padded, 3 + shift, 3 + shift + count, axis=2)

    return (
        0.75 * (take(1) - take(-1))
        - 0.15 * (take(2) - take(-2))
        + 1.0 / 60.0 * (take(3) - take(-3))
    )


def widened_x(fields):
    cells = fields.shape[1]
    blocks = lax.axis_size(GX)
    block = lax.axis_index(GX)
    total = cells * blocks
    margin = 14
    reach = margin + 2
    span = cells + 2 * margin
    padded = extended(fields, ((GX, 1),), reach)

    def take(shift):
        return padded[:, 2 + shift : 2 + shift + span]

    inner = 7.0 / 9.0 * (take(1) - take(-1)) + 1.0 / 36.0 * (take(2) - take(-2))
    first_row = 0.5 * (4.0 * take(1) + take(2) - 5.0 * take(0))
    second_row = 0.75 * (take(1) - take(-1))
    last_row = 0.5 * (5.0 * take(0) - 4.0 * take(-1) - take(-2))
    global_row = (block * cells - margin + jnp.arange(span, dtype=jnp.int32))[None, :, None, None]
    rhs = jnp.where(global_row == total - 1, last_row, inner)
    rhs = jnp.where(global_row == total - 2, second_row, rhs)
    rhs = jnp.where(global_row == 1, second_row, rhs)
    rhs = jnp.where(global_row == 0, first_row, rhs)
    whole = diagonals(total)
    lower_table = jnp.pad(whole[0], margin)
    middle_table = jnp.pad(whole[1], margin, constant_values=1.0)
    upper_table = jnp.pad(whole[2], margin)
    begin = block * cells
    lower = lax.dynamic_slice_in_dim(lower_table, begin, span).at[0].set(0.0)
    middle = lax.dynamic_slice_in_dim(middle_table, begin, span)
    upper = lax.dynamic_slice_in_dim(upper_table, begin, span).at[span - 1].set(0.0)
    inverse = inverse_of(lower, middle, upper)
    kept = inverse[margin : margin + cells]
    return jnp.einsum("ij,fjab->fiab", kept, rhs, precision=highest)


def per_device(state, mean_flow, face_cell, face_normal, face_pos, observer_pos, time_bin):
    cells, width, depth = (state.shape[1], state.shape[2], state.shape[3])
    fields = jnp.concatenate([state, mean_flow[None]], 0)
    x_rates = widened_x(fields)
    crossing = extended(fields[0::2], ((YZ, 2),), 3)
    y_rates = explicit_y(crossing, width)
    z_fields = jnp.concatenate([fields[0:1], fields[3:5]], 0)
    z_inverse = inverse_of(*diagonals(depth))
    z_rates = jnp.dot(compact_rhs(z_fields, 3), z_inverse.T, precision=highest)
    pressure, stream, lateral, vertical = (state[0], state[1], state[2], state[3])
    pressure_rate = -(mean_flow * x_rates[0] + x_rates[1] + y_rates[1] + z_rates[1])
    stream_rate = -(
        mean_flow * x_rates[1]
        + stream * x_rates[4]
        + lateral * y_rates[2]
        + vertical * z_rates[2]
        + x_rates[0]
    )
    lateral_rate = -(mean_flow * x_rates[2] + y_rates[0])
    vertical_rate = -(mean_flow * x_rates[3] + z_rates[0])
    rates = jnp.stack([pressure_rate, stream_rate, lateral_rate, vertical_rate])
    state_next = state + time_step * rates
    planes = width * lax.axis_size(YZ)
    block = lax.axis_index(GX)
    group = lax.axis_index(YZ)
    along_x = face_cell // (planes * depth) - block * cells
    along_y = face_cell // depth % planes - group * width
    along_z = face_cell % depth
    local_cell = (along_x * width + along_y) * depth + along_z
    face_rates = rates.reshape(4, -1)[:, local_cell]
    face_pressure = state_next[0].reshape(-1)[local_cell]
    normal_rate = (
        face_normal[0] * face_rates[1]
        + face_normal[1] * face_rates[2]
        + face_normal[2] * face_rates[3]
    )
    offset_x = observer_pos[0][None, :] - face_pos[0][:, None]
    offset_y = observer_pos[1][None, :] - face_pos[1][:, None]
    offset_z = observer_pos[2][None, :] - face_pos[2][:, None]
    distance = jnp.sqrt(offset_x * offset_x + offset_y * offset_y + offset_z * offset_z)
    normal_r = (
        face_normal[0][:, None] * offset_x
        + face_normal[1][:, None] * offset_y
        + face_normal[2][:, None] * offset_z
    ) / distance
    contribution = (
        normal_rate[:, None]
        + (face_rates[0][:, None] + face_pressure[:, None] / distance) * normal_r
    ) / (four_pi * distance)
    onehot = (time_bin[:, :, None] == jnp.arange(BINS, dtype=jnp.int32)).astype(jnp.float32)
    signal = sum_by_axis_2(
        jnp.sum(contribution[:, :, None] * onehot, axis=0), GX_YZ, (3, 0, 1, 2), 0
    )
    return (state_next, signal)


def solution(mesh):
    split = Mesh(mesh.devices.reshape(4, 4, 4, 2), ("gx_0", "gx_1", "yz_0", "yz_1"))
    return jax.shard_map(
        per_device,
        mesh=split,
        in_specs=(
            P(None, GX, YZ, None),
            P(GX, YZ, None),
            P(GX_YZ),
            P(None, GX_YZ),
            P(None, GX_YZ),
            P(),
            P(GX_YZ, None),
        ),
        out_specs=(P(None, GX, YZ, None), P(GX_YZ, None)),
        check_vma=False,
    )
```

profile of v0, /device:TPU:0, one launch (start us, length us, event | category | flops | bytes accessed | tf_op | source)
XLA Modules:
  0.0 1254.5 jit_solution(10763624095562554471)
XLA Ops:
  7.2 6.5 fusion.14
  13.7 5.6 collective-permute-start
  22.1 2.1 copy-done.4
  25.1 2.2 collective-permute-start.3
  41.4 457.6 %while.10 = (s32[]{:T(128)}, f32[]{:T(128)}, f32[256]{0:T(256)S(1)}, f32[7,32]{1,0:T(8,128)S(1)}, f32[7,32,256]{2,1,0:T(8,128)S(1)}, /*index=5*/f32[7,32]{1,0:T(...) while((s32[]{:T(128)}, f32[]{:T(128)}, ...), condition=%wide.region_1.2_spmd, body=%wide.region_0.1_spmd.sunk | while | flops 24705 | bytes 269033 | solution.py:68
  84.7 20.1 %subtract_divide_fusion.180 = (f32[256]{0:T(256)S(1)}, f32[256]{0:T(256)S(1)}, f32[256]{0:T(256)S(1)}, f32[256]{0:T(256)S(1)}, f32[256]{0:T(256)S(1)}, /*index=5...) fusion(f32[256]{0:T(256)S(1)} %bitcast.1797, ...), kind=kLoop, calls=%fused_computation.37.clone.1 | loop fusion | flops 24576 | bytes 66816 | tf_op jit(solution)/shard_map/while/body/eval_jaxpr/div | solution.py:68
  150.0 20.1 %subtract_divide_fusion.180 = (f32[256]{0:T(256)S(1)}, f32[256]{0:T(256)S(1)}, f32[256]{0:T(256)S(1)}, f32[256]{0:T(256)S(1)}, f32[256]{0:T(256)S(1)}, /*index=5...) fusion(f32[256]{0:T(256)S(1)} %bitcast.1797, ...), kind=kLoop, calls=%fused_computation.37.clone.1 | loop fusion | flops 24576 | bytes 66816 | tf_op jit(solution)/shard_map/while/body/eval_jaxpr/div | solution.py:68
  215.4 20.1 %subtract_divide_fusion.180 = (f32[256]{0:T(256)S(1)}, f32[256]{0:T(256)S(1)}, f32[256]{0:T(256)S(1)}, f32[256]{0:T(256)S(1)}, f32[256]{0:T(256)S(1)}, /*index=5...) fusion(f32[256]{0:T(256)S(1)} %bitcast.1797, ...), kind=kLoop, calls=%fused_computation.37.clone.1 | loop fusion | flops 24576 | bytes 66816 | tf_op jit(solution)/shard_map/while/body/eval_jaxpr/div | solution.py:68
  280.7 20.1 %subtract_divide_fusion.180 = (f32[256]{0:T(256)S(1)}, f32[256]{0:T(256)S(1)}, f32[256]{0:T(256)S(1)}, f32[256]{0:T(256)S(1)}, f32[256]{0:T(256)S(1)}, /*index=5...) fusion(f32[256]{0:T(256)S(1)} %bitcast.1797, ...), kind=kLoop, calls=%fused_computation.37.clone.1 | loop fusion | flops 24576 | bytes 66816 | tf_op jit(solution)/shard_map/while/body/eval_jaxpr/div | solution.py:68
  346.1 20.1 %subtract_divide_fusion.180 = (f32[256]{0:T(256)S(1)}, f32[256]{0:T(256)S(1)}, f32[256]{0:T(256)S(1)}, f32[256]{0:T(256)S(1)}, f32[256]{0:T(256)S(1)}, /*index=5...) fusion(f32[256]{0:T(256)S(1)} %bitcast.1797, ...), kind=kLoop, calls=%fused_computation.37.clone.1 | loop fusion | flops 24576 | bytes 66816 | tf_op jit(solution)/shard_map/while/body/eval_jaxpr/div | solution.py:68
  411.5 20.1 %subtract_divide_fusion.180 = (f32[256]{0:T(256)S(1)}, f32[256]{0:T(256)S(1)}, f32[256]{0:T(256)S(1)}, f32[256]{0:T(256)S(1)}, f32[256]{0:T(256)S(1)}, /*index=5...) fusion(f32[256]{0:T(256)S(1)} %bitcast.1797, ...), kind=kLoop, calls=%fused_computation.37.clone.1 | loop fusion | flops 24576 | bytes 66816 | tf_op jit(solution)/shard_map/while/body/eval_jaxpr/div | solution.py:68
  476.8 20.1 %subtract_divide_fusion.180 = (f32[256]{0:T(256)S(1)}, f32[256]{0:T(256)S(1)}, f32[256]{0:T(256)S(1)}, f32[256]{0:T(256)S(1)}, f32[256]{0:T(256)S(1)}, /*index=5...) fusion(f32[256]{0:T(256)S(1)} %bitcast.1797, ...), kind=kLoop, calls=%fused_computation.37.clone.1 | loop fusion | flops 24576 | bytes 66816 | tf_op jit(solution)/shard_map/while/body/eval_jaxpr/div | solution.py:68
  500.5 5.2 fusion.144
  506.6 2.5 pad_maximum_fusion.2
  509.1 6.3 fusion.25
  627.6 38.9 %fusion.134 = (f32[1,60]{1,0:T(1,128)}, f32[60]{0:T(128)}, f32[60]{0:T(128)}, f32[60]{0:T(128)}, f32[1,60]{1,0:T(1,128)S(1)}) fusion(f32[]{:T(128)S(6)} %div.5080, f32[]{:T(128)S(6)} %sub.6155, f32[]{:T(128)} %bitcast.436, f32[60,60]{1,0:T(8,128)S(1)} %fusion.54, f32[]{:T(128)S(6)} %div.5122, f32[]{:T(128)S(6)} %sub.6153, f32[]{:T(128)} %bitcast.433, ...), kind=kLoop, calls=%fused_computation.536 | loop fusion | flops 12480 | bytes 16136 | tf_op jit(solution)/shard_map/while/body/broadcast_in_dim | solution.py:68
  666.5 23.5 %subtract_divide_fusion.63 = (f32[1,60]{1,0:T(1,128)}, f32[1,60]{1,0:T(1,128)}, f32[1,60]{1,0:T(1,128)}, f32[1,60]{1,0:T(1,128)}, f32[1,60]{1,0:T(1,128)}, /*ind...) fusion(f32[60,60]{1,0:T(8,128)S(1)} %fusion.54, ...), kind=kLoop, calls=%fused_computation.503 | loop fusion | flops 6480 | bytes 15888 | tf_op jit(solution)/shard_map/eval_jaxpr/div | solution.py:68
  728.4 19.3 %subtract_divide_fusion.32 = (f32[256]{0:T(256)S(1)}, f32[256]{0:T(256)S(1)}, f32[256]{0:T(256)S(1)}, f32[256]{0:T(256)S(1)}, f32[256]{0:T(256)S(1)}, /*index=5*...) fusion(f32[256]{0:T(256)S(1)} %bitcast.1999, ...), kind=kLoop, calls=%fused_computation.319 | loop fusion | flops 23808 | bytes 64760 | tf_op jit(solution)/shard_map/eval_jaxpr/div | solution.py:68
  749.3 176.3 %while.11 = (s32[]{:T(128)}, f32[256]{0:T(256)S(1)}, f32[7,32,256]{2,1,0:T(8,128)S(1)}, f32[7,32,256]{2,1,0:T(8,128)S(1)}, f32[7,32]{1,0:T(8,128)}, /*index=5*/s...) while((s32[]{:T(128)}, f32[256]{0:T(256)S(1)}, ...), condition=%wide.region_3.4_spmd, body=%wide.region_2.3_spmd.sunk | while | flops 16418 | bytes 266713 | solution.py:68
  752.2 21.6 %multiply_subtract_fusion.185 = (f32[256]{0:T(256)}, f32[256]{0:T(256)S(1)}, f32[256]{0:T(256)S(1)}, f32[256]{0:T(256)S(1)}, f32[256]{0:T(256)S(1)}, /*index=5*/...) fusion(f32[256]{0:T(256)} %bitcast.1846, ...), kind=kLoop, calls=%fused_computation.103.clone.1 | loop fusion | flops 16384 | bytes 66688 | tf_op jit(solution)/shard_map/while/body/eval_jaxpr/sub | solution.py:68
  777.4 21.6 %multiply_subtract_fusion.185 = (f32[256]{0:T(256)}, f32[256]{0:T(256)S(1)}, f32[256]{0:T(256)S(1)}, f32[256]{0:T(256)S(1)}, f32[256]{0:T(256)S(1)}, /*index=5*/...) fusion(f32[256]{0:T(256)} %bitcast.1846, ...), kind=kLoop, calls=%fused_computation.103.clone.1 | loop fusion | flops 16384 | bytes 66688 | tf_op jit(solution)/shard_map/while/body/eval_jaxpr/sub | solution.py:68
  802.6 21.6 %multiply_subtract_fusion.185 = (f32[256]{0:T(256)}, f32[256]{0:T(256)S(1)}, f32[256]{0:T(256)S(1)}, f32[256]{0:T(256)S(1)}, f32[256]{0:T(256)S(1)}, /*index=5*/...) fusion(f32[256]{0:T(256)} %bitcast.1846, ...), kind=kLoop, calls=%fused_computation.103.clone.1 | loop fusion | flops 16384 | bytes 66688 | tf_op jit(solution)/shard_map/while/body/eval_jaxpr/sub | solution.py:68
  827.7 21.6 %multiply_subtract_fusion.185 = (f32[256]{0:T(256)}, f32[256]{0:T(256)S(1)}, f32[256]{0:T(256)S(1)}, f32[256]{0:T(256)S(1)}, f32[256]{0:T(256)S(1)}, /*index=5*/...) fusion(f32[256]{0:T(256)} %bitcast.1846, ...), kind=kLoop, calls=%fused_computation.103.clone.1 | loop fusion | flops 16384 | bytes 66688 | tf_op jit(solution)/shard_map/while/body/eval_jaxpr/sub | solution.py:68
  852.9 21.6 %multiply_subtract_fusion.185 = (f32[256]{0:T(256)}, f32[256]{0:T(256)S(1)}, f32[256]{0:T(256)S(1)}, f32[256]{0:T(256)S(1)}, f32[256]{0:T(256)S(1)}, /*index=5*/...) fusion(f32[256]{0:T(256)} %bitcast.1846, ...), kind=kLoop, calls=%fused_computation.103.clone.1 | loop fusion | flops 16384 | bytes 66688 | tf_op jit(solution)/shard_map/while/body/eval_jaxpr/sub | solution.py:68
  878.1 21.6 %multiply_subtract_fusion.185 = (f32[256]{0:T(256)}, f32[256]{0:T(256)S(1)}, f32[256]{0:T(256)S(1)}, f32[256]{0:T(256)S(1)}, f32[256]{0:T(256)S(1)}, /*index=5*/...) fusion(f32[256]{0:T(256)} %bitcast.1846, ...), kind=kLoop, calls=%fused_computation.103.clone.1 | loop fusion | flops 16384 | bytes 66688 | tf_op jit(solution)/shard_map/while/body/eval_jaxpr/sub | solution.py:68
  903.3 21.6 %multiply_subtract_fusion.185 = (f32[256]{0:T(256)}, f32[256]{0:T(256)S(1)}, f32[256]{0:T(256)S(1)}, f32[256]{0:T(256)S(1)}, f32[256]{0:T(256)S(1)}, /*index=5*/...) fusion(f32[256]{0:T(256)} %bitcast.1846, ...), kind=kLoop, calls=%fused_computation.103.clone.1 | loop fusion | flops 16384 | bytes 66688 | tf_op jit(solution)/shard_map/while/body/eval_jaxpr/sub | solution.py:68
  925.7 13.3 %pad_slice_fusion.12 = (f32[3,32,48,256]{3,2,1,0:T(8,128)}, f32[3,32,48,256]{3,2,1,0:T(8,128)}, f32[3,32,48,256]{3,2,1,0:T(8,128)}, f32[3,32,48,256]{3,2,1,0:T(8,128)}) fusion(f32[3,32,48,256]{3,2,1,0:T(8,128)} %pad_maximum_fusion.2), kind=kLoop, calls=%fused_computation.157 | loop fusion | bytes 23592960 | tf_op jit(solution)/shard_map/slice | solution.py:77
  939.0 2.5 copy.184
  941.4 2.5 copy.185
  943.9 2.5 copy.186
  946.4 2.3 copy.152
  948.7 2.3 copy.153
  951.0 2.5 copy.181
  953.5 2.5 copy.182
  956.8 2.3 copy.150
  959.1 2.2 copy.151
  961.3 10.5 fusion.5
  972.1 10.4 concatenate.77
  982.9 11.7 multiply_subtract_fusion.65
  994.7 19.3 %multiply_subtract_fusion.32 = (f32[256]{0:T(256)S(1)}, f32[256]{0:T(256)S(1)}, f32[256]{0:T(256)S(1)}, f32[256]{0:T(256)S(1)}, f32[256]{0:T(256)S(1)}, /*index=...) fusion(f32[256]{0:T(256)S(1)} %bitcast.1964, ...), kind=kLoop, calls=%fused_computation.288 | loop fusion | flops 15872 | bytes 64636 | tf_op jit(solution)/shard_map/eval_jaxpr/sub | solution.py:68
  1016.0 9.7 fusion.12
  1027.2 5.5 constant_dynamic-update-slice_fusion.1
  1032.8 5.0 fusion.8
  1037.9 9.8 pad_maximum_fusion.1
  1047.7 30.7 %fusion.2 = f32[5,60,48,256]{3,2,1,0:T(8,128)} fusion(f32[5,64,48,256]{3,2,1,0:T(8,128)} %pad_maximum_fusion.1, pred[60]{0:T(512)(128)(4,1)S(1)} %get-tuple-element.988, pred[60]{0:T(512)(128)(4,1)S(1)} %get-tuple-element.989, pred[60]{0:T(512)(128)(4,1)S(1)} %get-tuple-element.990, pred[60]{0:T(512)(128)(4,1)S(1)} %get-tuple-element.991), kind=kLoop, calls=%fused_computation.145 | loop fusion | flops 70041600 | bytes 88473840 | tf_op jit(solution)/shard_map/jit(_where)/select_n | solution.py:126
  1078.3 24.7 %fusion.17 = f32[5,32,48,256]{3,1,2,0:T(8,128)S(1)} fusion(f32[5,60,48,256]{3,2,1,0:T(8,128)} %fusion.2, f32[32,60]{1,0:T(8,128)S(1)} %concatenate.73), kind=kOutput, calls=%fused_computation.188 | convolution fusion | flops 1415577600 | bytes 22617600 | tf_op jit(solution)/shard_map/ij,fjab->fiab/dot_general | solution.py:137
  1103.1 9.3 fusion.41
  1113.5 2.1 copy.167
  1115.6 4.3 stack.30
  1119.9 3.6 copy.168
  1123.5 4.1 stack.31
  1127.7 2.1 copy.169
  1129.7 4.2 stack.32
  1135.9 4.2 stack.33
  1140.2 9.3 pad_maximum_fusion.3
  1149.4 4.3 gather_fusion
  1154.4 2.6 copy.163
  1157.0 2.5 copy.164
  1162.7 2.7 copy-done.8
  1168.8 7.5 select_reduce_fusion
  1177.2 15.7 %reduce-scatter.4.cloned.1.call-done = f32[64,4,64]{2,0,1:T(8,128)} async-done(((f32[128,4,64]{2,0,1:T(8,128)}), f32[64,4,64]{2,0,1:T(8,128)}) %reduce-scatter.4.cloned.1.call-update) | async-done | bytes 65552 | tf_op jit(solution)/shard_map/reduce_scatter | solution.py:36
  1194.9 22.9 %reduce-scatter.6.cloned.1.call-done = f32[16,4,64]{2,0,1:T(8,128)} async-done(((f32[64,4,64]{2,0,1:T(8,128)}), f32[16,4,64]{2,0,1:T(8,128)}) %reduce-scatter.6.cloned.1.call-update) | async-done | bytes 16400 | tf_op jit(solution)/shard_map/reduce_scatter | solution.py:36
  1217.8 17.6 %all-reduce.4 = f32[16,4,64]{2,0,1:T(8,128)S(1)} all-reduce(f32[16,4,64]{2,0,1:T(8,128)} %reduce-scatter.6.cloned.1.call-done), channel_id=4, replica_groups=mesh['gx_0'=4,'gx_1'=4,'yz_0'=4,'yz_1'=2] {'gx_1'}, use_global_device_ids=true, to_apply=%region_7.8.clone | all-reduce | flops 4096 | bytes 32768
  1235.4 10.6 all-reduce.5
  (376 shorter events, 93.0 us)
Async XLA Ops:
  7.2 1185.8 %reduce-scatter.4.cloned.1.call-start = ((), (), s32[]{:S(2)}) async-start(), calls=%async_computation.2 | async-start | bytes 393216 | tf_op jit(solution)/shard_map/reduce_scatter | solution.py:36
  7.2 13.4 %copy-start = (f32[4,32,48,256]{3,2,1,0:T(8,128)S(1)}, f32[4,32,48,256]{3,2,1,0:T(8,128)}, u32[]{:S(2)}) copy-start(f32[4,32,48,256]{3,2,1,0:T(8,128)} %param.15) | copy-start | bytes 18874372
  7.2 13.4 %copy-start.1 = (f32[32,48,256]{2,1,0:T(8,128)S(1)}, f32[32,48,256]{2,1,0:T(8,128)}, u32[]{:S(2)}) copy-start(f32[32,48,256]{2,1,0:T(8,128)} %param.16) | copy-start | bytes 4718596
  13.7 1024.2 %collective-permute-start = (f32[5,16,48,256]{3,2,1,0:T(8,128)}, f32[5,16,48,256]{3,2,1,0:T(8,128)}, u32[]{:S(2)}, u32[]{:S(2)}) collective-permute-start(f32[5,16,48,256]{3,2,1,0:T(8,128)} %get-tuple-element.615), channel_id=1, source_target_pairs={{0,8},{8,16},{16,24},{24,32},{32,40},{40,48},{48,56},{56,64},{64,7... | collective-permute-start | bytes 11796488 | tf_op jit(solution)/shard_map/ppermute | solution.py:23
  19.4 1018.5 %collective-permute-start.1 = (f32[5,16,48,256]{3,2,1,0:T(8,128)}, f32[5,16,48,256]{3,2,1,0:T(8,128)}, u32[]{:S(2)}, u32[]{:S(2)}) collective-permute-start(f32[5,16,48,256]{3,2,1,0:T(8,128)} %get-tuple-element.616), channel_id=1, source_target_pairs={{8,0},{16,8},{24,16},{32,24},{40,32},{48,40},{56,48},{64,56},{72,6... | collective-permute-start | bytes 11796488 | tf_op jit(solution)/shard_map/ppermute | solution.py:26
  25.1 1001.1 %collective-permute-start.3 = (f32[3,32,3,256]{3,1,2,0:T(8,128)}, f32[3,32,3,256]{3,1,2,0:T(8,128)}, u32[]{:S(2)}, u32[]{:S(2)}) collective-permute-start(f32[3,32,3,256]{3,1,2,0:T(8,128)} %copy.206), channel_id=1, source_target_pairs={{0,1},{1,2},{2,3},{3,4},{4,5},{5,6},{6,7},{8,9},{9,10},{10,11},{11... | collective-permute-start | bytes 884744 | tf_op jit(solution)/shard_map/ppermute | solution.py:23
  28.1 1004.7 %collective-permute-start.2 = (f32[3,32,3,256]{3,1,2,0:T(8,128)}, f32[3,32,3,256]{3,1,2,0:T(8,128)S(1)}, u32[]{:S(2)}, u32[]{:S(2)}) collective-permute-start(f32[3,32,3,256]{3,1,2,0:T(8,128)} %copy.207), channel_id=1, source_target_pairs={{1,0},{2,1},{3,2},{4,3},{5,4},{6,5},{7,6},{9,8},{10,9},{11,10},{12... | collective-permute-start | bytes 884744 | tf_op jit(solution)/shard_map/ppermute | solution.py:26
  41.4 464.3 %slice-start = ((s8[6291456]{0:T(1024)(128)(4,1)}), s8[2097152]{0:T(1024)(128)(4,1)S(1)}, s32[]{:S(2)}) async-start(s8[6291456]{0:T(1024)(128)(4,1)} %bitcast.1706), calls=%async_computation.4 | async-start | bytes 4194304
  500.5 5.3 slice-start.1
  500.5 5.7 copy-start.2
  953.4 7.8 copy-start.20
  953.4 7.8 copy-start.60
  953.5 7.8 copy-start.61
  961.3 10.5 copy-start.9
  971.8 10.8 copy-start.32
  971.8 10.8 copy-start.33
  971.8 10.8 copy-start.34
  971.8 10.8 copy-start.35
  971.9 10.8 copy-start.36
  971.9 10.8 copy-start.37
  971.9 10.8 copy-start.38
  971.9 10.8 copy-start.39
  971.9 10.8 copy-start.40
  971.9 10.8 copy-start.41
  971.9 10.8 copy-start.42
  971.9 10.8 copy-start.43
  971.9 10.8 copy-start.44
  971.9 10.8 copy-start.45
  972.0 10.8 copy-start.46
  972.0 10.8 copy-start.47
  972.0 10.8 copy-start.48
  972.0 10.8 copy-start.49
  972.0 10.8 copy-start.50
  972.0 10.8 copy-start.51
  972.0 10.8 copy-start.52
  972.0 10.8 copy-start.53
  972.0 10.8 copy-start.54
  972.0 10.8 copy-start.55
  972.1 10.8 copy-start.56
  972.1 10.8 copy-start.57
  972.1 10.8 copy-start.58
  972.1 10.8 copy-start.59
  972.1 22.5 %copy-start.31 = (f32[1,60]{1,0:T(1,128)S(1)}, f32[1,60]{1,0:T(1,128)}, u32[]{:S(2)}) copy-start(f32[1,60]{1,0:T(1,128)} %get-tuple-element.325) | copy-start | bytes 724
  972.1 42.0 %copy-start.62 = (s32[192]{0:T(256)S(1)}, s32[192]{0:T(256)}, u32[]{:S(2)}) copy-start(s32[192]{0:T(256)} %param.17) | copy-start | bytes 2308
  972.1 42.6 %copy-start.29 = (f32[3,192]{1,0:T(4,128)S(1)}, f32[3,192]{1,0:T(4,128)}, u32[]{:S(2)}) copy-start(f32[3,192]{1,0:T(4,128)} %param.18) | copy-start | bytes 6916
  972.1 43.2 %copy-start.30 = (f32[3,192]{1,0:T(4,128)S(1)}, f32[3,192]{1,0:T(4,128)}, u32[]{:S(2)}) copy-start(f32[3,192]{1,0:T(4,128)} %param.19) | copy-start | bytes 6916
  1016.0 9.7 copy-start.21
  1027.2 10.6 slice-start.2
  1032.8 5.1 slice-start.3
  1032.8 5.1 copy-start.3
  1078.3 24.7 %copy-start.5 = (f32[3,32,48,256]{3,1,2,0:T(8,128)S(1)}, f32[3,32,48,256]{3,1,2,0:T(8,128)}, u32[]{:S(2)}) copy-start(f32[3,32,48,256]{3,1,2,0:T(8,128)} %fusion.8) | copy-start | bytes 14155780
  1078.3 24.7 %copy-start.10 = (f32[1,32,48,256]{3,2,1,0:T(8,128)S(1)}, f32[1,32,48,256]{3,2,1,0:T(8,128)}, u32[]{:S(2)}) copy-start(f32[1,32,48,256]{3,2,1,0:T(8,128)} %get-tuple-element.617) | copy-start | bytes 4718596
  1078.3 24.7 %copy-start.11 = (f32[1,32,48,256]{3,2,1,0:T(8,128)S(1)}, f32[1,32,48,256]{3,2,1,0:T(8,128)}, u32[]{:S(2)}) copy-start(f32[1,32,48,256]{3,2,1,0:T(8,128)} %get-tuple-element.618) | copy-start | bytes 4718596
  1078.3 24.7 %copy-start.12 = (f32[1,32,48,256]{3,2,1,0:T(8,128)S(1)}, f32[1,32,48,256]{3,2,1,0:T(8,128)}, u32[]{:S(2)}) copy-start(f32[1,32,48,256]{3,2,1,0:T(8,128)} %get-tuple-element.620) | copy-start | bytes 4718596
  1115.6 12.0 copy-start.6
  1140.2 9.3 copy-start.16
  1153.8 7.6 slice-start.4
  1157.0 4.3 slice-start.5
  1165.4 2.8 copy-start.17
  1165.5 2.8 copy-start.18
  1165.5 3.3 copy-start.13
  1165.5 27.5 %copy-start.64 = (u32[128]{0:T(128)S(1)}, u32[128]{0:T(128)}, u32[]{:S(2)}) copy-start(u32[128]{0:T(128)} %constant.279) | copy-start | bytes 1540
  1165.5 28.1 %copy-start.63 = (u32[128]{0:T(128)S(1)}, u32[128]{0:T(128)}, u32[]{:S(2)}) copy-start(u32[128]{0:T(128)} %constant.283) | copy-start | bytes 1540
  1177.2 40.6 %reduce-scatter.6.cloned.1.call-start = ((), (), s32[]{:S(2)}) async-start(), calls=%async_computation.3 | async-start | bytes 163840 | tf_op jit(solution)/shard_map/reduce_scatter | solution.py:36
  (13 other events, 33.9 us)
Sparse Core Ops, SparseCore 0:
  1177.3 15.6 reduce-scatter.3
  1195.3 22.4 reduce-scatter.5
where the time goes:
time: 1280 us; the launch traced here: 1250 us
  other arithmetic  505 us (39%)
  loops' own time  290 us (23%)
  local copies, waits for them, and re-layouts  181 us (14%)
  between operations  167 us (13%)
  waiting for transfers between devices  38.7 us (3%)
  matrix products  34.3 us (3%)
  blocking collectives  28.2 us (2%)
    another operation x2, loops' own time, inverse_of(): lax.linalg.tridiagonal_solve(lower, middle, upper, jnp.eye(count, dtype=j...  290 us
    div x9, other arithmetic, inverse_of(): lax.linalg.tridiagonal_solve(lower, middle, upper, jnp.eye(count, dtype=j...  183 us
    sub x9, other arithmetic, inverse_of(): lax.linalg.tridiagonal_solve(lower, middle, upper, jnp.eye(count, dtype=j...  182 us
    slice x97, local copies, waits for them, and re-layouts, inverse_of(): lax.linalg.tridiagonal_solve(lower, middle, upper, jnp.eye(count, dtype=j...  49.4 us
    broadcast_in_dim x3, other arithmetic, inverse_of(): lax.linalg.tridiagonal_solve(lower, middle, upper, jnp.eye(count, dtype=j...  38.9 us
    reduce_scatter x2, waiting for transfers between devices, sum_in_order(): pieces = lax.psum_scatter(pieces, axes[k], scatter_dimension=0, tiled=True)  38.7 us
    select_n x1, other arithmetic, widened_x(): rhs = jnp.where(global_row == 0, first_row, rhs)  30.7 us
    unnamed x156, local copies, waits for them, and re-layouts  30 us
  transfers between devices with their start and end apart: 6, of which 2 were waited for; matrix products, arithmetic and copies ran while one was open for 46% of the time, Pallas kernels for 0%

commit v1 on v0

v1 whole, which is shorter than its diff:
```python
import functools

import jax
import jax.numpy as jnp
import numpy as np
from jax import lax
from jax.experimental import pallas as pl
from jax.experimental.pallas import tpu as pltpu
from jax.sharding import PartitionSpec as P

CX, CY, NZ = 32, 48, 256
FACES_DEV, OBS, BINS = 192, 512, 64
N_GX, N_YZ = 16, 8
TIME_STEP = 0.25
INV_FOUR_PI = 1.0 / (4.0 * 3.141592653589793)
MESH = pl.DeviceIdType.MESH
F32, BF16 = jnp.float32, jnp.bfloat16

LAM = (-1.0 + np.sqrt(1.0 - 4.0 / 9.0)) / (2.0 / 3.0)
CC, DD = 25.0 / 12.0, -1.0 / 12.0
CL = CC * LAM
KK = DD / CL


def operator(n):
    a = np.eye(n)
    b = np.zeros((n, n))
    for i in range(n):
        if i == 0:
            a[0, 1] = 2.0
            b[0, :3] = (-2.5, 2.0, 0.5)
        elif i == n - 1:
            a[i, i - 1] = 2.0
            b[i, n - 3 :] = (-0.5, -2.0, 2.5)
        elif i in (1, n - 2):
            a[i, i - 1] = a[i, i + 1] = 0.25
            b[i, i + 1], b[i, i - 1] = 0.75, -0.75
        else:
            a[i, i - 1] = a[i, i + 1] = 1.0 / 3.0
            b[i, i + 1], b[i, i - 1] = 7.0 / 9.0, -7.0 / 9.0
            b[i, i + 2], b[i, i - 2] = 1.0 / 36.0, -1.0 / 36.0
    return np.linalg.solve(a, b)


def closure(n, total):
    lag = np.arange(n)[:, None] - np.arange(n)[None, :]
    inside = np.where(
        lag == 0, 0.0, np.sign(lag) * (CC * LAM ** np.abs(lag) + DD * (np.abs(lag) == 1))
    )
    rest = operator(total)[:n, :n] - inside
    factors = np.stack([CC * LAM ** (np.arange(n) + 1.0), DD * (np.arange(n) == 0)], 1)
    return np.linalg.lstsq(factors, rest, rcond=None)[0]


def split2(x):
    hi = x.astype(BF16)
    return hi, (x - hi.astype(F32)).astype(BF16)


def dot3(a, b):
    return (
        jnp.dot(a[0], b[0], preferred_element_type=F32)
        + jnp.dot(a[1], b[0], preferred_element_type=F32)
        + jnp.dot(a[0], b[1], preferred_element_type=F32)
    )


def kernel(
    ends, state, mean, face_cell, normal, pos, obs, tbin, dz, table, table_s_in,
    nxt, sig,
    fld, grd, hal, tsum, stg, geo, tbp, face_v, normal_v, pos_v, obs_v, tbin_v, dz_v, table_v,
    rows_v, binned, packed, recv_a, send_b, recv_b, table_s, cell_s,
    ld_sem, in_sem, xs_sem, xr_sem, ys_sem, yr_sem, as_sem, ar_sem, bs_sem, br_sem,
):
    gx = lax.axis_index("gx")
    yz = lax.axis_index("yz")

    order = (0, 2, 4, 1, 3)
    loads = {}
    for f in order:
        src = mean if f == 4 else state.at[f]
        for t in range(2):
            c = pltpu.make_async_copy(
                src.at[:, :, pl.ds(128 * t, 128)], fld.at[f, :, t, pl.ds(8, CY), :], ld_sem.at[f, t]
            )
            c.start()
            loads[f, t] = c
    small = []
    for k, (s, d) in enumerate((
        (dz, dz_v), (table, table_v), (table_s_in, table_s), (face_cell, cell_s),
        (face_cell, face_v), (normal, normal_v), (pos, pos_v), (obs, obs_v), (tbin, tbin_v),
    )):
        c = pltpu.make_async_copy(s, d, in_sem.at[k])
        c.start()
        small.append(c)

    barrier = pltpu.get_barrier_semaphore()
    for k in range(1, N_GX):
        pl.semaphore_signal(barrier, inc=1, device_id=(lax.rem(gx + k, N_GX), yz), device_id_type=MESH)
    for k in range(1, N_YZ):
        pl.semaphore_signal(barrier, inc=1, device_id=(gx, lax.rem(yz + k, N_YZ)), device_id_type=MESH)
    pl.semaphore_wait(barrier, N_GX + N_YZ - 2)

    has_left, has_right = gx > 0, gx < N_GX - 1
    has_low, has_high = yz > 0, yz < N_YZ - 1
    right, left = (lax.rem(gx + 1, N_GX), yz), (lax.rem(gx + N_GX - 1, N_GX), yz)
    high, low = (gx, lax.rem(yz + 1, N_YZ)), (gx, lax.rem(yz + N_YZ - 1, N_YZ))

    def xcopy(src, dst, way, k):
        return pltpu.make_async_remote_copy(
            src_ref=src, dst_ref=dst, send_sem=xs_sem.at[way, k], recv_sem=xr_sem.at[way, k],
            device_id=(right, left)[way], device_id_type=MESH,
        )

    xc = ([], [])
    for way, plane in ((0, CX - 1), (1, 0)):
        xc[way].append(xcopy(state.at[:, plane], hal.at[pl.ds(0, 4), 2 + way], way, 0))
        xc[way].append(xcopy(mean.at[plane], hal.at[4, 2 + way], way, 1))
        for f in range(5):
            xc[way].append(xcopy(tsum.at[way, f], hal.at[f, way], way, 2 + f))
    sends = (has_right, has_left)
    gets = (has_left, has_right)
    for way in range(2):
        @pl.when(sends[way])
        def _():
            xc[way][0].start()
            xc[way][1].start()

    yc = ([], [])
    for k, f in enumerate((0, 2, 4)):
        for way, (first, there) in enumerate(((8 + CY - 3, 5), (8, 8 + CY))):
            yc[way].append(pltpu.make_async_remote_copy(
                src_ref=fld.at[f, :, :, pl.ds(first, 3), :], dst_ref=fld.at[f, :, :, pl.ds(there, 3), :],
                send_sem=ys_sem.at[way, k], recv_sem=yr_sem.at[way, k],
                device_id=(high, low)[way], device_id_type=MESH,
            ))
    ysends = (has_high, has_low)
    ygets = (has_low, has_high)

    for n_done, f in enumerate(order):
        loads[f, 0].wait()
        loads[f, 1].wait()
        if f in (0, 2, 4):
            for way in range(2):
                @pl.when(ysends[way])
                def _():
                    yc[way][f // 2].start()

        def sweep(t, _):
            zero = jnp.zeros((CY, 128), F32)
            acc, edge = zero, zero
            for i in range(CX):
                grd[f, i, t] = edge
                v = fld[f, i, t, pl.ds(8, CY), :]
                acc = LAM * acc + v
                edge = acc + KK * v
            tsum[0, f, :, pl.ds(pl.multiple_of(128 * t, 128), 128)] = acc
            acc, edge = zero, zero
            for i in reversed(range(CX)):
                grd[f, i, t] = CL * (grd[f, i, t] - edge)
                v = fld[f, i, t, pl.ds(8, CY), :]
                acc = LAM * acc + v
                edge = acc + KK * v
            tsum[1, f, :, pl.ds(pl.multiple_of(128 * t, 128), 128)] = acc
            return 0

        lax.fori_loop(0, 2, sweep, 0)
        for way in range(2):
            @pl.when(sends[way])
            def _():
                xc[way][2 + f].start()

    for way, there in ((0, jnp.logical_not(has_left)), (1, jnp.logical_not(has_right))):
        @pl.when(there)
        def _():
            def close(n, _):
                f, t = n // 2, n % 2
                one = jnp.zeros((CY, 128), F32)
                two = jnp.zeros((CY, 128), F32)
                for i in range(CX):
                    v = fld[f, i if way == 0 else CX - 1 - i, t, pl.ds(8, CY), :]
                    one = one + float(ends[0, i]) * v
                    two = two + float(ends[1, i]) * v
                lanes = pl.ds(pl.multiple_of(128 * t, 128), 128)
                hal[f, way, :, lanes] = one
                hal[f, 2 + way, :, lanes] = two
                return 0

            lax.fori_loop(0, 10, close, 0)
    for way, there, row in ((0, jnp.logical_not(has_low), 5), (1, jnp.logical_not(has_high), 8 + CY)):
        @pl.when(there)
        def _():
            for f in (0, 2, 4):
                fld[f, :, :, pl.ds(row, 3), :] = jnp.zeros((CX, 2, 3, 128), F32)

    for c in small:
        c.wait()
    for way in range(2):
        @pl.when(ygets[way])
        def _():
            for k in range(3):
                yc[way][k].wait_recv()

    dz_hi, dz_lo = dz_v[0], dz_v[1]
    step = 4

    def local(n, _):
        x0 = n * step
        zs = []
        for f in (0, 3, 4):
            v = fld[f, pl.ds(x0, step), :, pl.ds(8, CY), :]
            v = jnp.concatenate([v[:, 0], v[:, 1]], axis=-1).reshape(step * CY, NZ)
            zs.append(dot3(split2(v), (dz_hi, dz_lo)))
        for j in range(step):
            for t in range(2):
                x = x0 + j
                at = lambda f, s=0: fld[f, x, t, pl.ds(8 + s, CY), :]
                pz, wz, mz = (a[j * CY : (j + 1) * CY, 128 * t : 128 * t + 128] for a in zs)

                def dy(f):
                    return (
                        0.75 * (at(f, 1) - at(f, -1)) - 0.15 * (at(f, 2) - at(f, -2))
                        + (1.0 / 60.0) * (at(f, 3) - at(f, -3))
                    )

                px, ux, vx, wx, mx = (grd[f, x, t] for f in range(5))
                m, u, v, w = at(4), at(1), at(2), at(3)
                grd[0, x, t] = m * px + ux + dy(2) + wz
                grd[1, x, t] = m * ux + u * mx + v * dy(4) + w * mz + px
                grd[2, x, t] = m * vx + dy(0)
                grd[3, x, t] = m * wx + pz
        return 0

    lax.fori_loop(0, CX // step, local, 0)

    def gather(n, _):
        for k in range(8):
            j = n * 8 + k
            cell = cell_s[0, j]
            line = lax.shift_right_logical(cell, 8)
            x = lax.shift_right_logical(lax.shift_right_logical(line, 7) * 21846, 16)
            y = line - CY * lax.shift_right_logical(lax.shift_right_logical(line, 4) * 21846, 16)
            x = x & (CX - 1)
            t = lax.shift_right_logical(cell, 7) & 1
            for q in range(4):
                stg[q, pl.ds(j, 1), :] = grd[q, x, t, pl.ds(y, 1), :]
            for q, f in ((4, 0), (5, 1), (6, 4)):
                stg[q, pl.ds(j, 1), :] = fld[f, x, t, pl.ds(8 + y, 1), :]
        return 0

    lax.fori_loop(0, FACES_DEV // 8, gather, 0)

    cell = face_v[...]
    line = lax.shift_right_logical(cell, 8)
    fx = lax.shift_right_logical(lax.shift_right_logical(line, 7) * 21846, 16)
    fy = line - CY * lax.shift_right_logical(lax.shift_right_logical(line, 4) * 21846, 16)
    fx = fx & (CX - 1)
    fz = cell & 255
    rows_v[...] = jnp.zeros((16, 256), F32)
    rows_v[pl.ds(0, 3), pl.ds(0, FACES_DEV)] = pos_v[...]
    rows_v[pl.ds(3, 3), pl.ds(0, FACES_DEV)] = normal_v[...]
    rows_v[pl.ds(6, 1), pl.ds(0, FACES_DEV)] = fx.astype(F32)
    rows_v[pl.ds(7, 1), pl.ds(0, FACES_DEV)] = fy.astype(F32)
    rows_v[pl.ds(8, 1), pl.ds(0, FACES_DEV)] = fz.astype(F32)
    cols = rows_v[...].T
    col = lambda k: cols[:FACES_DEV, k : k + 1]
    xcol, ycol, zcol = col(6), col(7), col(8)
    lane = lax.broadcasted_iota(jnp.int32, (FACES_DEV, 128), 1).astype(F32)
    zlane = zcol - jnp.where(zcol >= 128.0, 128.0, 0.0)
    zmask = zlane == lane
    pick = lambda a: jnp.sum(jnp.where(zmask, a, 0.0), axis=1, keepdims=True)
    face0 = [pick(stg[q]) for q in range(7)]
    xmask = xcol == lane
    coef = [
        jnp.sum(jnp.where(xmask, table_v[pl.ds(k, 1), :], 0.0), axis=1, keepdims=True) for k in range(4)
    ]
    wide = lax.broadcasted_iota(jnp.int32, (FACES_DEV, 4 * CY), 1)
    part = (wide >= CY).astype(jnp.int32) + (wide >= 2 * CY).astype(jnp.int32) + (wide >= 3 * CY).astype(jnp.int32)
    hit = (wide - CY * part).astype(F32) == ycol
    weight = jnp.where(
        hit,
        jnp.where(part == 0, coef[0], jnp.where(part == 1, coef[1], jnp.where(part == 2, coef[2], coef[3]))),
        0.0,
    )
    weight = split2(weight)

    to = lax.broadcasted_iota(jnp.int32, (OBS, OBS), 1)
    source = (
        32 * (lax.shift_right_logical(to, 1) & 15) + 4 * (lax.shift_right_logical(to, 5) & 7)
        + 2 * (to & 1) + lax.shift_right_logical(to, 8)
    )
    perm = jnp.where(lax.broadcasted_iota(jnp.int32, (OBS, OBS), 0) == source, 1.0, 0.0).astype(BF16)
    tbp[...] = jnp.dot(tbin_v[...].astype(F32).astype(BF16), perm, preferred_element_type=F32)
    whole = obs_v[...]
    o_hi = whole.astype(BF16)
    rest = whole - o_hi.astype(F32)
    o_mid = rest.astype(BF16)
    o_lo = (rest - o_mid.astype(F32)).astype(BF16)
    seen = (
        jnp.dot(o_hi, perm, preferred_element_type=F32)
        + jnp.dot(o_mid, perm, preferred_element_type=F32)
        + jnp.dot(o_lo, perm, preferred_element_type=F32)
    )
    for t in range(4):
        lanes = slice(128 * t, 128 * t + 128)
        dx = seen[0:1, lanes] - col(0)
        dy_ = seen[1:2, lanes] - col(1)
        dz_ = seen[2:3, lanes] - col(2)
        inv = lax.rsqrt(dx * dx + dy_ * dy_ + dz_ * dz_)
        nr = (col(3) * dx + col(4) * dy_ + col(5) * dz_) * inv
        q1 = INV_FOUR_PI * inv
        geo[0, :, lanes] = q1
        geo[1, :, lanes] = q1 * nr
        geo[2, :, lanes] = q1 * nr * inv

    for way in range(2):
        @pl.when(gets[way])
        def _():
            for k in range(7):
                xc[way][k].wait_recv()
    near = []
    for f in range(5):
        near.append(dot3(weight, split2(hal[f].reshape(4 * CY, NZ))))
    fp, fu, fm = face0[4], face0[5], face0[6]
    add0 = fm * near[0] + near[1]
    adda = (
        col(3) * (fm * near[1] + fu * near[4] + near[0])
        + (col(4) * fm) * near[2] + (col(5) * fm) * near[3]
    )
    zwide = lax.broadcasted_iota(jnp.int32, (FACES_DEV, NZ), 1).astype(F32) == zcol
    pickw = lambda a: jnp.sum(jnp.where(zwide, a, 0.0), axis=1, keepdims=True)
    rate0 = -(face0[0] + pickw(add0))
    ratea = -(col(3) * face0[1] + col(4) * face0[2] + col(5) * face0[3] + pickw(adda))
    pnext = fp + TIME_STEP * rate0
    for t in range(4):
        lanes = slice(128 * t, 128 * t + 128)
        geo[0, :, lanes] = ratea * geo[0, :, lanes] + rate0 * geo[1, :, lanes] + pnext * geo[2, :, lanes]

    def one_bin(b, _):
        want = b.astype(F32)
        for t in range(4):
            acc = jnp.zeros((8, 128), F32)
            for g in range(FACES_DEV // 8):
                rows = pl.ds(8 * g, 8)
                lanes = pl.ds(128 * t, 128)
                acc = acc + jnp.where(tbp[rows, lanes] == want, geo[0, rows, lanes], 0.0)
            binned[t, pl.ds(b, 1), :] = jnp.sum(acc, axis=0, keepdims=True)
        return 0

    lax.fori_loop(0, BINS, one_bin, 0)
    for t in range(2):
        both = jnp.concatenate([binned[t], binned[2 + t]], axis=0)
        packed[pl.ds(128 * t, 128), :] = both.T

    ac = []
    for k in range(1, N_YZ):
        peer = lax.rem(yz + k, N_YZ)
        c = pltpu.make_async_remote_copy(
            src_ref=packed.at[pl.ds(pl.multiple_of(32 * peer, 32), 32), :], dst_ref=recv_a.at[k - 1],
            send_sem=as_sem.at[k - 1], recv_sem=ar_sem.at[k - 1], device_id=(gx, peer), device_id_type=MESH,
        )
        c.start()
        ac.append(c)

    def finish(x, _):
        ca, cb = table_s[0, x], table_s[1, x]
        for t in range(2):
            for h in range(2):
                lanes = pl.ds(128 * t, 128)
                ys = pl.ds(24 * h, 24)
                px, ux, vx, wx, mx = (ca * hal[f, 0, ys, lanes] + cb * hal[f, 1, ys, lanes] for f in range(5))
                p, u, v, w, m = (fld[f, x, t, pl.ds(8 + 24 * h, 24), :] for f in range(5))
                n0, n1, n2, n3 = (grd[q, x, t, ys, :] for q in range(4))
                nxt[0, x, ys, lanes] = p - TIME_STEP * (n0 + m * px + ux)
                nxt[1, x, ys, lanes] = u - TIME_STEP * (n1 + m * ux + u * mx + px)
                nxt[2, x, ys, lanes] = v - TIME_STEP * (n2 + m * vx)
                nxt[3, x, ys, lanes] = w - TIME_STEP * (n3 + m * wx)
        return 0

    def edges():
        for x, k, sign in ((0, 2, DD), (CX - 1, 3, -DD)):
            for t in range(2):
                lanes = pl.ds(128 * t, 128)
                px, ux, vx, wx, mx = ((-TIME_STEP * sign) * hal[f, k, :, lanes] for f in range(5))
                u, m = fld[1, x, t, pl.ds(8, CY), :], fld[4, x, t, pl.ds(8, CY), :]
                nxt[0, x, :, lanes] += m * px + ux
                nxt[1, x, :, lanes] += m * ux + u * mx + px
                nxt[2, x, :, lanes] += m * vx
                nxt[3, x, :, lanes] += m * wx

    lax.fori_loop(0, CX // 2, finish, 0)

    total = packed[pl.ds(pl.multiple_of(32 * yz, 32), 32), :]
    for k in range(N_YZ - 1):
        ac[k].wait_recv()
        total = total + recv_a[k]
    for g in range(N_GX):
        send_b[g] = total[2 * g : 2 * g + 2]
    bc = []
    for k in range(1, N_GX):
        peer = lax.rem(gx + k, N_GX)
        c = pltpu.make_async_remote_copy(
            src_ref=send_b.at[peer], dst_ref=recv_b.at[k - 1],
            send_sem=bs_sem.at[k - 1], recv_sem=br_sem.at[k - 1], device_id=(peer, yz), device_id_type=MESH,
        )
        c.start()
        bc.append(c)

    lax.fori_loop(CX // 2, CX, finish, 0)
    edges()

    total = send_b[gx]
    for k in range(N_GX - 1):
        bc[k].wait_recv()
        total = total + recv_b[k]
    for h in range(2):
        for h2 in range(2):
            sig[pl.ds(2 * h + h2, 1), :] = total[h : h + 1, BINS * h2 : BINS * h2 + BINS]

    for way in range(2):
        @pl.when(sends[way])
        def _():
            for c in xc[way]:
                c.wait_send()

        @pl.when(ysends[way])
        def _():
            for c in yc[way]:
                c.wait_send()
    for c in ac + bc:
        c.wait_send()


def per_device(state, mean_flow, face_cell, face_normal, face_pos, observer_pos, time_bin):
    n = np.arange(CX)
    table = np.zeros((8, 128), np.float32)
    table[0, :CX] = CC * LAM ** (n + 1.0)
    table[1, :CX] = -CC * LAM ** (CX - n * 1.0)
    table[2, 0] = DD
    table[3, CX - 1] = -DD
    dz = operator(NZ).T.astype(np.float32)
    dz = jnp.stack(split2(jnp.asarray(dz)))
    ends = closure(CX, CX * N_GX)
    anywhere = pl.BlockSpec(memory_space=pl.ANY)
    vm = pltpu.VMEM
    dma = pltpu.SemaphoreType.DMA
    nxt, sig = pl.pallas_call(
        functools.partial(kernel, ends),
        out_shape=(
            jax.ShapeDtypeStruct((4, CX, CY, NZ), F32),
            jax.ShapeDtypeStruct((4, BINS), F32),
        ),
        in_specs=[anywhere] * 10,
        out_specs=(pl.BlockSpec(memory_space=pltpu.VMEM), pl.BlockSpec(memory_space=pltpu.VMEM)),
        scratch_shapes=[
            vm((5, CX, 2, 64, 128), F32),
            vm((5, CX, 2, CY, 128), F32),
            vm((5, 4, CY, NZ), F32),
            vm((2, 5, CY, NZ), F32),
            vm((7, FACES_DEV, 128), F32),
            vm((3, FACES_DEV, OBS), F32),
            vm((FACES_DEV, OBS), F32),
            vm((1, FACES_DEV), jnp.int32),
            vm((3, FACES_DEV), F32),
            vm((3, FACES_DEV), F32),
            vm((3, OBS), F32),
            vm((FACES_DEV, OBS), jnp.int32),
            vm((2, NZ, NZ), BF16),
            vm((8, 128), F32),
            vm((16, 256), F32),
            vm((4, BINS, 128), F32),
            vm((256, 128), F32),
            vm((N_YZ - 1, 32, 128), F32),
            vm((N_GX, 2, 128), F32),
            vm((N_GX - 1, 2, 128), F32),
            pltpu.SMEM((4, 128), F32),
            pltpu.SMEM((1, FACES_DEV), jnp.int32),
            dma((5, 2)), dma((9,)), dma((2, 7)), dma((2, 7)), dma((2, 3)), dma((2, 3)),
            dma((N_YZ - 1,)), dma((N_YZ - 1,)), dma((N_GX - 1,)), dma((N_GX - 1,)),
        ],
        compiler_params=pltpu.CompilerParams(
            collective_id=0, has_side_effects=True, vmem_limit_bytes=63000 * 1024
        ),
    )(
        state, mean_flow, face_cell.reshape(1, FACES_DEV), face_normal, face_pos, observer_pos, time_bin,
        dz, jnp.asarray(table), jnp.asarray(table[:4]),
    )
    return nxt, sig


def solution(mesh):
    return jax.shard_map(
        per_device,
        mesh=mesh,
        in_specs=(
            P(None, "gx", "yz", None),
            P("gx", "yz", None),
            P(("gx", "yz")),
            P(None, ("gx", "yz")),
            P(None, ("gx", "yz")),
            P(),
            P(("gx", "yz"), None),
        ),
        out_specs=(P(None, "gx", "yz", None), P(("gx", "yz"), None)),
        check_vma=False,
    )
```

time: 1280 us -> 46 us (0.04); the launches traced: 1250 us -> 45.5 us
  other arithmetic: 505 us -> 0 us
  loops' own time: 290 us -> 0 us
  local copies, waits for them, and re-layouts: 181 us -> 6.55 us
  between operations: 167 us -> 0.65 us
  waiting for transfers between devices: 38.7 us -> 0 us
  Pallas kernels: 0 us -> 38.3 us
  matrix products: 34.3 us -> 0 us
  blocking collectives: 28.2 us -> 0 us
    another operation x2 -> x0, loops' own time: 290 us -> none  [inverse_of(): lax.linalg.tridiagonal_solve(lower, middle, upper, jnp.eye(count, dtype=j...]
    div x10 -> x0, other arithmetic: 184 us -> none  [the longest x9 183 us: inverse_of(): lax.linalg.tridiagonal_solve(lower, middle, upper, jnp.eye(count, dtype=j...]
    sub x9 -> x0, other arithmetic: 182 us -> none  [inverse_of(): lax.linalg.tridiagonal_solve(lower, middle, upper, jnp.eye(count, dtype=j...]
    slice x106 -> x0, local copies, waits for them, and re-layouts: 70.9 us -> none  [the longest x97 49.4 us: inverse_of(): lax.linalg.tridiagonal_solve(lower, middle, upper, jnp.eye(count, dtype=j...]
    broadcast_in_dim x3 -> x0, other arithmetic: 38.9 us -> none  [inverse_of(): lax.linalg.tridiagonal_solve(lower, middle, upper, jnp.eye(count, dtype=j...]
    reduce_scatter x2 -> x0, waiting for transfers between devices: 38.7 us -> none  [sum_in_order(): pieces = lax.psum_scatter(pieces, axes[k], scatter_dimension=0, tiled=True)]
    pallas_call x0 -> x1, Pallas kernels: none -> 38.3 us  [per_device(): pl.pallas_call(functools.partial(kernel, ends), out_shape=(jax.ShapeDtype...]
    dot_general x2 -> x0, matrix products: 34.3 us -> none  [the longest x1 24.7 us: widened_x(): return jnp.einsum('ij,fjab->fiab', kept, rhs, precision=highest)]
  transfers between devices with their start and end apart: 6 -> 0, of which waited for: 2 -> 0; matrix products, arithmetic and copies ran while one was open for 46% -> 0% of each run, Pallas kernels for 0% -> 0%
where the time goes in v1:
time: 46 us; the launch traced here: 45.5 us
  Pallas kernels  38.3 us (83%)
  local copies, waits for them, and re-layouts  6.55 us (14%)
  between operations  0.65 us (1%)
    pallas_call x1, Pallas kernels, per_device(): pl.pallas_call(functools.partial(kernel, ends), out_shape=(jax.ShapeDtype...  38.3 us
    unnamed x4, local copies, waits for them, and re-layouts  6.55 us

profile of v1, /device:TPU:0, one launch (start us, length us, event | category | flops | bytes accessed | tf_op | source)
XLA Modules:
  0.0 45.5 jit_solution(7581600389768620543)
XLA Ops:
  0.6 38.3 %shard_map.113 = (f32[4,32,48,256]{3,2,1,0:T(8,128)}, f32[4,64]{1,0:T(4,128)}) custom-call(f32[4,32,48,256]{3,2,1,0:T(8,128)} %state.1, f32[32,48,256]{2,1,0:T(8,128)} %mean.1, s32[1,192]{1,0:T(1,128)} %bitcast.1, f32[3,192]{1,0:T(4,128)} %normal.1, f32[3,192]{1,0:T(4,128)} %pos.1, f32[3,512]{1,0:T(4,128)} %obs.1, s32[192,512]{1,0:T(8,128)} %tbin.1, ...), custom_call_target="tpu_custom_call" | custom-call | tf_op jit(solution)/shard_map/pallas_call | solution.py:447
  38.9 0.0 copy-start
  38.9 6.0 %copy.14 = f32[4,32,48,256]{3,2,1,0:T(8,128)} copy(f32[4,32,48,256]{3,2,1,0:T(8,128)} %get-tuple-element.4) | data formatting | bytes 12582912
  44.9 0.0 copy-done
  44.9 0.6 %copy.15 = f32[4,64]{1,0:T(4,128)} copy(f32[4,64]{1,0:T(4,128)S(1)} %copy-done) | data formatting | bytes 2048
Async XLA Ops:
  38.9 6.0 %copy-start = (f32[4,64]{1,0:T(4,128)S(1)}, f32[4,64]{1,0:T(4,128)}, u32[]{:S(2)}) copy-start(f32[4,64]{1,0:T(4,128)} %get-tuple-element.5) | copy-start | bytes 3076

commit v2 on v1

--- a/solution.py
+++ b/solution.py
@@ -18,8 +18,7 @@
 
 LAM = (-1.0 + np.sqrt(1.0 - 4.0 / 9.0)) / (2.0 / 3.0)
 CC, DD = 25.0 / 12.0, -1.0 / 12.0
-CL = CC * LAM
-KK = DD / CL
+EDGE = DD / CC
 
 
 def operator(n):
@@ -49,12 +48,26 @@
     )
     rest = operator(total)[:n, :n] - inside
     factors = np.stack([CC * LAM ** (np.arange(n) + 1.0), DD * (np.arange(n) == 0)], 1)
-    return np.linalg.lstsq(factors, rest, rcond=None)[0]
+    weights = np.linalg.lstsq(factors, rest, rcond=None)[0]
+    scale = weights[:, 12] / LAM**12
+    return np.concatenate([weights[:, :4] - scale[:, None] * LAM ** np.arange(4.0), scale[:, None]], 1)
 
 
 def split2(x):
     hi = x.astype(BF16)
     return hi, (x - hi.astype(F32)).astype(BF16)
+
+
+class Marks:
+    def __init__(self):
+        self.scope = None
+
+    def __call__(self, name):
+        if self.scope is not None:
+            self.scope.__exit__(None, None, None)
+        self.scope = None if name is None else jax.named_scope(name)
+        if self.scope is not None:
+            self.scope.__enter__()
 
 
 def dot3(a, b):
@@ -66,16 +79,27 @@
 
 
 def kernel(
-    ends, state, mean, face_cell, normal, pos, obs, tbin, dz, table, table_s_in,
+    ends, state, mean, face_cell, normal, pos, obs, tbin, dz, table, table_s_in, had,
     nxt, sig,
-    fld, grd, hal, tsum, stg, geo, tbp, face_v, normal_v, pos_v, obs_v, tbin_v, dz_v, table_v,
-    rows_v, binned, packed, recv_a, send_b, recv_b, table_s, cell_s,
+    fld, grd, zed, hal, tsum, stg, geo, sgn, face_v, normal_v, pos_v, obs_v, tbin_v, dz_v, table_v, had_v,
+    rows_v, seen_v, binned, packed, recv_a, send_b, recv_b, table_s, cell_s,
     ld_sem, in_sem, xs_sem, xr_sem, ys_sem, yr_sem, as_sem, ar_sem, bs_sem, br_sem,
 ):
+    mark = Marks()
     gx = lax.axis_index("gx")
     yz = lax.axis_index("yz")
 
-    order = (0, 2, 4, 1, 3)
+    mark("start")
+    order = (0, 4, 2, 3, 1)
+    small = []
+    for k, (s, d) in enumerate((
+        (obs, obs_v), (tbin, tbin_v), (dz, dz_v), (table, table_v), (table_s_in, table_s),
+        (face_cell, cell_s), (face_cell, face_v), (normal, normal_v), (pos, pos_v), (had, had_v),
+    )):
+        c = pltpu.make_async_copy(s, d, in_sem.at[k])
+        c.start()
+        small.append(c)
+
     loads = {}
     for f in order:
         src = mean if f == 4 else state.at[f]
@@ -85,22 +109,38 @@
             )
             c.start()
             loads[f, t] = c
-    small = []
-    for k, (s, d) in enumerate((
-        (dz, dz_v), (table, table_v), (table_s_in, table_s), (face_cell, cell_s),
-        (face_cell, face_v), (normal, normal_v), (pos, pos_v), (obs, obs_v), (tbin, tbin_v),
-    )):
-        c = pltpu.make_async_copy(s, d, in_sem.at[k])
-        c.start()
-        small.append(c)
-
+    mark("barrier")
     barrier = pltpu.get_barrier_semaphore()
     for k in range(1, N_GX):
         pl.semaphore_signal(barrier, inc=1, device_id=(lax.rem(gx + k, N_GX), yz), device_id_type=MESH)
     for k in range(1, N_YZ):
         pl.semaphore_signal(barrier, inc=1, device_id=(gx, lax.rem(yz + k, N_YZ)), device_id_type=MESH)
+    mark("observers")
+    to = lax.broadcasted_iota(jnp.int32, (OBS, OBS), 1)
+    source = (
+        32 * (lax.shift_right_logical(to, 1) & 15) + 4 * (lax.shift_right_logical(to, 5) & 7)
+        + 2 * (to & 1) + lax.shift_right_logical(to, 8)
+    )
+    perm = jnp.where(lax.broadcasted_iota(jnp.int32, (OBS, OBS), 0) == source, 1.0, 0.0).astype(BF16)
+    small[0].wait()
+    small[1].wait()
+    which = jnp.dot(tbin_v[...].astype(F32).astype(BF16), perm, preferred_element_type=F32).astype(jnp.int32)
+    for k in range(6):
+        sgn[k] = jnp.where((which & (1 << k)) == 0, 1.0, -1.0)
+    whole = obs_v[...]
+    o_hi = whole.astype(BF16)
+    rest = whole - o_hi.astype(F32)
+    o_mid = rest.astype(BF16)
+    o_lo = (rest - o_mid.astype(F32)).astype(BF16)
+    seen_v[pl.ds(0, 3), :] = (
+        jnp.dot(o_hi, perm, preferred_element_type=F32)
+        + jnp.dot(o_mid, perm, preferred_element_type=F32)
+        + jnp.dot(o_lo, perm, preferred_element_type=F32)
+    )
+    mark("barrier_wait")
     pl.semaphore_wait(barrier, N_GX + N_YZ - 2)
 
+    mark("issue")
     has_left, has_right = gx > 0, gx < N_GX - 1
     has_low, has_high = yz > 0, yz < N_YZ - 1
     right, left = (lax.rem(gx + 1, N_GX), yz), (lax.rem(gx + N_GX - 1, N_GX), yz)
@@ -137,7 +177,21 @@
     ysends = (has_high, has_low)
     ygets = (has_low, has_high)
 
-    for n_done, f in enumerate(order):
+    mark("sweeps")
+    small[2].wait()
+
+    def along_z(j):
+        q = j // 4
+        x0 = 8 * (j - 4 * q)
+        f = jnp.where(q == 0, 0, 5 - q)
+        v = fld[f, pl.ds(x0, 8), :, pl.ds(8, CY), :]
+        v = jnp.concatenate([v[:, 0], v[:, 1]], axis=-1).reshape(8 * CY, NZ)
+        hi, lo = split2(v)
+        out = jnp.dot(jnp.concatenate([hi, lo, hi], axis=1), dz_v[...], preferred_element_type=F32)
+        zed[q, pl.ds(x0, 8)] = out.reshape(8, CY, NZ)
+
+    jobs = 0
+    for f, per_half in zip(order, (1, 1, 1, 2, 1)):
         loads[f, 0].wait()
         loads[f, 1].wait()
         if f in (0, 2, 4):
@@ -146,42 +200,50 @@
                 def _():
                     yc[way][f // 2].start()
 
-        def sweep(t, _):
+        def sweep(t, _, f=f, per_half=per_half, jobs=jobs):
             zero = jnp.zeros((CY, 128), F32)
-            acc, edge = zero, zero
+            at = lambda i: fld[f, i, t, pl.ds(8, CY), :] if 0 <= i < CX else zero
+            up, down, v_old, w_old = zero, zero, zero, zero
+            v, w = at(0), at(CX - 1)
             for i in range(CX):
-                grd[f, i, t] = edge
-                v = fld[f, i, t, pl.ds(8, CY), :]
-                acc = LAM * acc + v
-                edge = acc + KK * v
-            tsum[0, f, :, pl.ds(pl.multiple_of(128 * t, 128), 128)] = acc
-            acc, edge = zero, zero
-            for i in reversed(range(CX)):
-                grd[f, i, t] = CL * (grd[f, i, t] - edge)
-                v = fld[f, i, t, pl.ds(8, CY), :]
-                acc = LAM * acc + v
-                edge = acc + KK * v
-            tsum[1, f, :, pl.ds(pl.multiple_of(128 * t, 128), 128)] = acc
+                if i * per_half // CX != (i - 1) * per_half // CX:
+                    along_z(jobs + per_half * t + i * per_half // CX)
+                k = CX - 1 - i
+                v_new, w_new = at(i + 1), at(k - 1)
+                if i < CX // 2:
+                    grd[f, i, t, pl.ds(0, CY), :] = up
+                    grd[f, k, t, pl.ds(0, CY), :] = down
+                else:
+                    grd[f, i, t, pl.ds(0, CY), :] = (up - grd[f, i, t, pl.ds(0, CY), :]) + EDGE * (v_old - v_new)
+                    grd[f, k, t, pl.ds(0, CY), :] = (grd[f, k, t, pl.ds(0, CY), :] - down) + EDGE * (w_new - w_old)
+                up_sum, down_sum = up + v, down + w
+                up, down = LAM * up_sum, LAM * down_sum
+                v_old, v, w_old, w = v, v_new, w, w_new
+            lanes = pl.ds(pl.multiple_of(128 * t, 128), 128)
+            tsum[0, f, :, lanes] = up_sum
+            tsum[1, f, :, lanes] = down_sum
             return 0
 
         lax.fori_loop(0, 2, sweep, 0)
+        jobs += 2 * per_half
         for way in range(2):
             @pl.when(sends[way])
             def _():
                 xc[way][2 + f].start()
 
+    mark("ends")
     for way, there in ((0, jnp.logical_not(has_left)), (1, jnp.logical_not(has_right))):
         @pl.when(there)
         def _():
             def close(n, _):
                 f, t = n // 2, n % 2
-                one = jnp.zeros((CY, 128), F32)
-                two = jnp.zeros((CY, 128), F32)
-                for i in range(CX):
+                lanes = pl.ds(pl.multiple_of(128 * t, 128), 128)
+                far = tsum[1 - way, f, :, lanes]
+                one, two = float(ends[0, 4]) * far, float(ends[1, 4]) * far
+                for i in range(4):
                     v = fld[f, i if way == 0 else CX - 1 - i, t, pl.ds(8, CY), :]
                     one = one + float(ends[0, i]) * v
                     two = two + float(ends[1, i]) * v
-                lanes = pl.ds(pl.multiple_of(128 * t, 128), 128)
                 hal[f, way, :, lanes] = one
                 hal[f, 2 + way, :, lanes] = two
                 return 0
@@ -193,7 +255,8 @@
             for f in (0, 2, 4):
                 fld[f, :, :, pl.ds(row, 3), :] = jnp.zeros((CX, 2, 3, 128), F32)
 
-    for c in small:
+    mark("wait_y")
+    for c in small[3:]:
         c.wait()
     for way in range(2):
         @pl.when(ygets[way])
@@ -201,21 +264,13 @@
             for k in range(3):
                 yc[way][k].wait_recv()
 
-    dz_hi, dz_lo = dz_v[0], dz_v[1]
-    step = 4
-
+    mark("local")
     def local(n, _):
-        x0 = n * step
-        zs = []
-        for f in (0, 3, 4):
-            v = fld[f, pl.ds(x0, step), :, pl.ds(8, CY), :]
-            v = jnp.concatenate([v[:, 0], v[:, 1]], axis=-1).reshape(step * CY, NZ)
-            zs.append(dot3(split2(v), (dz_hi, dz_lo)))
-        for j in range(step):
+        for j in range(2):
             for t in range(2):
-                x = x0 + j
+                x = 2 * n + j
                 at = lambda f, s=0: fld[f, x, t, pl.ds(8 + s, CY), :]
-                pz, wz, mz = (a[j * CY : (j + 1) * CY, 128 * t : 128 * t + 128] for a in zs)
+                pz, mz, wz = (zed[q, x, :, 128 * t : 128 * t + 128] for q in range(3))
 
                 def dy(f):
                     return (
@@ -223,33 +278,38 @@
                         + (1.0 / 60.0) * (at(f, 3) - at(f, -3))
                     )
 
-                px, ux, vx, wx, mx = (grd[f, x, t] for f in range(5))
+                px, ux, vx, wx, mx = (grd[f, x, t, pl.ds(0, CY), :] for f in range(5))
                 m, u, v, w = at(4), at(1), at(2), at(3)
-                grd[0, x, t] = m * px + ux + dy(2) + wz
-                grd[1, x, t] = m * ux + u * mx + v * dy(4) + w * mz + px
-                grd[2, x, t] = m * vx + dy(0)
-                grd[3, x, t] = m * wx + pz
+                cm = CC * m
+                grd[0, x, t, pl.ds(0, CY), :] = cm * px + CC * ux + dy(2) + wz
+                grd[1, x, t, pl.ds(0, CY), :] = cm * ux + CC * (u * mx + px) + v * dy(4) + w * mz
+                grd[2, x, t, pl.ds(0, CY), :] = cm * vx + dy(0)
+                grd[3, x, t, pl.ds(0, CY), :] = cm * wx + pz
         return 0
 
-    lax.fori_loop(0, CX // step, local, 0)
+    lax.fori_loop(0, CX // 2, local, 0)
+
+    mark("gather")
+    corner = gx * (CX * CY * N_YZ) + yz * CY
+    grd_rows = grd.reshape(5, CX * 2 * 64, 128)
+    fld_rows = fld.reshape(5, CX * 2 * 64, 128)
 
     def gather(n, _):
         for k in range(8):
             j = n * 8 + k
             cell = cell_s[0, j]
-            line = lax.shift_right_logical(cell, 8)
-            x = lax.shift_right_logical(lax.shift_right_logical(line, 7) * 21846, 16)
-            y = line - CY * lax.shift_right_logical(lax.shift_right_logical(line, 4) * 21846, 16)
-            x = x & (CX - 1)
-            t = lax.shift_right_logical(cell, 7) & 1
+            line = jnp.maximum(lax.shift_right_logical(cell, 8) - corner, 0)
+            x = lax.shift_right_logical(lax.shift_right_logical(line, 7) * 86, 8)
+            row = line - 256 * x + (lax.shift_right_logical(cell, 1) & 64)
             for q in range(4):
-                stg[q, pl.ds(j, 1), :] = grd[q, x, t, pl.ds(y, 1), :]
+                stg[q, pl.ds(j, 1), :] = grd_rows[q, pl.ds(row, 1), :]
             for q, f in ((4, 0), (5, 1), (6, 4)):
-                stg[q, pl.ds(j, 1), :] = fld[f, x, t, pl.ds(8 + y, 1), :]
+                stg[q, pl.ds(j, 1), :] = fld_rows[f, pl.ds(row + 8, 1), :]
         return 0
 
     lax.fori_loop(0, FACES_DEV // 8, gather, 0)
 
+    mark("columns")
     cell = face_v[...]
     line = lax.shift_right_logical(cell, 8)
     fx = lax.shift_right_logical(lax.shift_right_logical(line, 7) * 21846, 16)
@@ -282,30 +342,15 @@
         jnp.where(part == 0, coef[0], jnp.where(part == 1, coef[1], jnp.where(part == 2, coef[2], coef[3]))),
         0.0,
     )
-    weight = split2(weight)
-
-    to = lax.broadcasted_iota(jnp.int32, (OBS, OBS), 1)
-    source = (
-        32 * (lax.shift_right_logical(to, 1) & 15) + 4 * (lax.shift_right_logical(to, 5) & 7)
-        + 2 * (to & 1) + lax.shift_right_logical(to, 8)
-    )
-    perm = jnp.where(lax.broadcasted_iota(jnp.int32, (OBS, OBS), 0) == source, 1.0, 0.0).astype(BF16)
-    tbp[...] = jnp.dot(tbin_v[...].astype(F32).astype(BF16), perm, preferred_element_type=F32)
-    whole = obs_v[...]
-    o_hi = whole.astype(BF16)
-    rest = whole - o_hi.astype(F32)
-    o_mid = rest.astype(BF16)
-    o_lo = (rest - o_mid.astype(F32)).astype(BF16)
-    seen = (
-        jnp.dot(o_hi, perm, preferred_element_type=F32)
-        + jnp.dot(o_mid, perm, preferred_element_type=F32)
-        + jnp.dot(o_lo, perm, preferred_element_type=F32)
-    )
+    hi, lo = split2(weight)
+    weight = jnp.concatenate([hi, lo, hi], axis=1)
+
+    mark("geometry")
     for t in range(4):
         lanes = slice(128 * t, 128 * t + 128)
-        dx = seen[0:1, lanes] - col(0)
-        dy_ = seen[1:2, lanes] - col(1)
-        dz_ = seen[2:3, lanes] - col(2)
+        dx = seen_v[0:1, lanes] - col(0)
+        dy_ = seen_v[1:2, lanes] - col(1)
+        dz_ = seen_v[2:3, lanes] - col(2)
         inv = lax.rsqrt(dx * dx + dy_ * dy_ + dz_ * dz_)
         nr = (col(3) * dx + col(4) * dy_ + col(5) * dz_) * inv
         q1 = INV_FOUR_PI * inv
@@ -313,14 +358,17 @@
         geo[1, :, lanes] = q1 * nr
         geo[2, :, lanes] = q1 * nr * inv
 
+    mark("wait_x")
     for way in range(2):
         @pl.when(gets[way])
         def _():
-            for k in range(7):
-                xc[way][k].wait_recv()
+            for c in xc[way]:
+                c.wait_recv()
+    mark("near")
     near = []
     for f in range(5):
-        near.append(dot3(weight, split2(hal[f].reshape(4 * CY, NZ))))
+        hi, lo = split2(hal[f].reshape(4 * CY, NZ))
+        near.append(jnp.dot(weight, jnp.concatenate([hi, hi, lo], axis=0), preferred_element_type=F32))
     fp, fu, fm = face0[4], face0[5], face0[6]
     add0 = fm * near[0] + near[1]
     adda = (
@@ -336,21 +384,48 @@
         lanes = slice(128 * t, 128 * t + 128)
         geo[0, :, lanes] = ratea * geo[0, :, lanes] + rate0 * geo[1, :, lanes] + pnext * geo[2, :, lanes]
 
-    def one_bin(b, _):
-        want = b.astype(F32)
-        for t in range(4):
-            acc = jnp.zeros((8, 128), F32)
-            for g in range(FACES_DEV // 8):
-                rows = pl.ds(8 * g, 8)
-                lanes = pl.ds(128 * t, 128)
-                acc = acc + jnp.where(tbp[rows, lanes] == want, geo[0, rows, lanes], 0.0)
-            binned[t, pl.ds(b, 1), :] = jnp.sum(acc, axis=0, keepdims=True)
+    mark("bins")
+    def patterns(n, _):
+        t = n // 8
+        block = n - 8 * t
+        lanes = pl.ds(pl.multiple_of(128 * t, 128), 128)
+        after = block + 1
+        bit = jnp.where(after % 2 == 1, 3, jnp.where(after % 4 == 2, 4, 5))
+        acc = [jnp.zeros((8, 128), F32)] * 8
+        for g in range(FACES_DEV // 8):
+            rows = pl.ds(8 * g, 8)
+            what = geo[0, rows, lanes]
+            geo[0, rows, lanes] = what * sgn[bit, rows, lanes]
+            low = [sgn[k, rows, lanes] for k in range(3)]
+            for k in range(8):
+                if k:
+                    what = what * low[0 if k % 2 else (1 if k % 4 else 2)]
+                acc[k] = acc[k] + what
+        for k in range(8):
+            binned[t, pl.ds(pl.multiple_of(64 * block, 8) + 8 * k, 8), :] = acc[k]
         return 0
 
-    lax.fori_loop(0, BINS, one_bin, 0)
+    lax.fori_loop(0, 32, patterns, 0)
+    mark("pack")
+
+    def folded(t):
+        out = binned[t, pl.ds(0, BINS, stride=8), :]
+        for k in range(1, 8):
+            out = out + binned[t, pl.ds(k, BINS, stride=8), :]
+        return out
+
     for t in range(2):
-        both = jnp.concatenate([binned[t], binned[2 + t]], axis=0)
-        packed[pl.ds(128 * t, 128), :] = both.T
+        both = jnp.concatenate([folded(t), folded(2 + t)], axis=0).T
+        hi = both.astype(BF16)
+        rest = both - hi.astype(F32)
+        mid = rest.astype(BF16)
+        lo = (rest - mid.astype(F32)).astype(BF16)
+        had = had_v[...]
+        packed[pl.ds(128 * t, 128), :] = (
+            jnp.dot(hi, had, preferred_element_type=F32)
+            + jnp.dot(mid, had, preferred_element_type=F32)
+            + jnp.dot(lo, had, preferred_element_type=F32)
+        )
 
     ac = []
     for k in range(1, N_YZ):
@@ -362,6 +437,7 @@
         c.start()
         ac.append(c)
 
+    mark("finish_a")
     def finish(x, _):
         ca, cb = table_s[0, x], table_s[1, x]
         for t in range(2):
@@ -390,6 +466,7 @@
 
     lax.fori_loop(0, CX // 2, finish, 0)
 
+    mark("wait_a")
     total = packed[pl.ds(pl.multiple_of(32 * yz, 32), 32), :]
     for k in range(N_YZ - 1):
         ac[k].wait_recv()
@@ -406,9 +483,11 @@
         c.start()
         bc.append(c)
 
+    mark("finish_b")
     lax.fori_loop(CX // 2, CX, finish, 0)
     edges()
 
+    mark("wait_b")
     total = send_b[gx]
     for k in range(N_GX - 1):
         bc[k].wait_recv()
@@ -417,6 +496,7 @@
         for h2 in range(2):
             sig[pl.ds(2 * h + h2, 1), :] = total[h : h + 1, BINS * h2 : BINS * h2 + BINS]
 
+    mark("drain")
     for way in range(2):
         @pl.when(sends[way])
         def _():
@@ -429,6 +509,7 @@
                 c.wait_send()
     for c in ac + bc:
         c.wait_send()
+    mark(None)
 
 
 def per_device(state, mean_flow, face_cell, face_normal, face_pos, observer_pos, time_bin):
@@ -439,51 +520,60 @@
     table[2, 0] = DD
     table[3, CX - 1] = -DD
     dz = operator(NZ).T.astype(np.float32)
-    dz = jnp.stack(split2(jnp.asarray(dz)))
+    dz_hi, dz_lo = split2(jnp.asarray(dz))
+    dz = jnp.concatenate([dz_hi, dz_hi, dz_lo], axis=0)
     ends = closure(CX, CX * N_GX)
-    anywhere = pl.BlockSpec(memory_space=pl.ANY)
+    gray = np.arange(BINS) // 8 * 8
+    gray = (gray ^ (gray >> 1) & 56) + ((n := np.arange(BINS) % 8) ^ (n >> 1))
+    common = gray[:, None] & np.arange(BINS)[None, :]
+    parity = sum((common >> k) & 1 for k in range(6)) % 2
+    had = np.kron(np.eye(2), (1.0 - 2.0 * parity) / BINS).astype(np.float32)
+    anywhere = pl.BlockSpec(memory_space=pltpu.HBM)
     vm = pltpu.VMEM
     dma = pltpu.SemaphoreType.DMA
     nxt, sig = pl.pallas_call(
         functools.partial(kernel, ends),
         out_shape=(
-            jax.ShapeDtypeStruct((4, CX, CY, NZ), F32),
-            jax.ShapeDtypeStruct((4, BINS), F32),
+            vm((4, CX, CY, NZ), F32),
+            vm((4, BINS), F32),
         ),
-        in_specs=[anywhere] * 10,
+        in_specs=[anywhere] * 11,
         out_specs=(pl.BlockSpec(memory_space=pltpu.VMEM), pl.BlockSpec(memory_space=pltpu.VMEM)),
         scratch_shapes=[
             vm((5, CX, 2, 64, 128), F32),
-            vm((5, CX, 2, CY, 128), F32),
+            vm((5, CX, 2, 64, 128), F32),
+            vm((3, CX, CY, NZ), F32),
             vm((5, 4, CY, NZ), F32),
             vm((2, 5, CY, NZ), F32),
             vm((7, FACES_DEV, 128), F32),
             vm((3, FACES_DEV, OBS), F32),
-            vm((FACES_DEV, OBS), F32),
+            vm((6, FACES_DEV, OBS), F32),
             vm((1, FACES_DEV), jnp.int32),
             vm((3, FACES_DEV), F32),
             vm((3, FACES_DEV), F32),
             vm((3, OBS), F32),
             vm((FACES_DEV, OBS), jnp.int32),
-            vm((2, NZ, NZ), BF16),
+            vm((3 * NZ, NZ), BF16),
             vm((8, 128), F32),
+            vm((128, 128), BF16),
             vm((16, 256), F32),
-            vm((4, BINS, 128), F32),
+            vm((8, OBS), F32),
+            vm((4, 8 * BINS, 128), F32),
             vm((256, 128), F32),
             vm((N_YZ - 1, 32, 128), F32),
             vm((N_GX, 2, 128), F32),
             vm((N_GX - 1, 2, 128), F32),
             pltpu.SMEM((4, 128), F32),
             pltpu.SMEM((1, FACES_DEV), jnp.int32),
-            dma((5, 2)), dma((9,)), dma((2, 7)), dma((2, 7)), dma((2, 3)), dma((2, 3)),
+            dma((5, 2)), dma((10,)), dma((2, 7)), dma((2, 7)), dma((2, 3)), dma((2, 3)),
             dma((N_YZ - 1,)), dma((N_YZ - 1,)), dma((N_GX - 1,)), dma((N_GX - 1,)),
         ],
         compiler_params=pltpu.CompilerParams(
-            collective_id=0, has_side_effects=True, vmem_limit_bytes=63000 * 1024
+            collective_id=0, has_side_effects=True, vmem_limit_bytes=57 * 2**20 + 2**19
         ),
     )(
         state, mean_flow, face_cell.reshape(1, FACES_DEV), face_normal, face_pos, observer_pos, time_bin,
-        dz, jnp.asarray(table), jnp.asarray(table[:4]),
+        dz, jnp.asarray(table), jnp.asarray(table[:4]), jnp.asarray(had, BF16),
     )
     return nxt, sig
 

time: 46 us -> 38.2 us (0.83)
  Pallas kernels: 38.3 us -> 33.8 us
  local copies, waits for them, and re-layouts: 6.55 us -> 3.28 us
    pallas_call x1, Pallas kernels: 38.3 us -> 33.8 us  [per_device(): pl.pallas_call(functools.partial(kernel, ends), out_shape=(vm((4, CX, CY,...]
    unnamed x4 -> x2, local copies, waits for them, and re-layouts: 6.55 us -> 3.28 us
where the time goes in v2:
time: 38.2 us; the launch traced here: 37.7 us
  Pallas kernels  33.8 us (88%)
  local copies, waits for them, and re-layouts  3.28 us (9%)
  between operations  0.64 us (2%)
    pallas_call x1, Pallas kernels, per_device(): pl.pallas_call(functools.partial(kernel, ends), out_shape=(vm((4, CX, CY,...  33.8 us
    unnamed x2, local copies, waits for them, and re-layouts  3.28 us

profile of v2, /device:TPU:0, one launch (start us, length us, event | category | flops | bytes accessed | tf_op | source)
XLA Modules:
  0.0 37.7 jit_solution(670990726041419832)
XLA Ops:
  0.6 33.8 %shard_map.122 = (f32[4,32,48,256]{3,2,1,0:T(8,128)S(1)}, f32[4,64]{1,0:T(4,128)S(1)}) custom-call(f32[4,32,48,256]{3,2,1,0:T(8,128)} %state.1, f32[32,48,256]{2,1,0:T(8,128)} %mean.1, s32[1,192]{1,0:T(1,128)} %bitcast.1, f32[3,192]{1,0:T(4,128)} %normal.1, f32[3,192]{1,0:T(4,128)} %pos.1, f32[3,512]{1,0:T(4,128)} %obs.1, s32[192,512]{1,0:T(8,128)} %tbin.1, ...), custom_call_target="tpu_custom_call" | custom-call | tf_op jit(solution)/shard_map/pallas_call | solution.py:534
  34.4 2.7 %copy.15 = f32[4,32,48,256]{3,2,1,0:T(8,128)} copy(f32[4,32,48,256]{3,2,1,0:T(8,128)S(1)} %get-tuple-element.2) | data formatting | bytes 12582912
  37.1 0.6 %copy.16 = f32[4,64]{1,0:T(4,128)} copy(f32[4,64]{1,0:T(4,128)S(1)} %get-tuple-element.3) | data formatting | bytes 2048

commit v3 on v2

--- a/solution.py
+++ b/solution.py
@@ -83,12 +83,33 @@
     nxt, sig,
     fld, grd, zed, hal, tsum, stg, geo, sgn, face_v, normal_v, pos_v, obs_v, tbin_v, dz_v, table_v, had_v,
     rows_v, seen_v, binned, packed, recv_a, send_b, recv_b, table_s, cell_s,
-    ld_sem, in_sem, xs_sem, xr_sem, ys_sem, yr_sem, as_sem, ar_sem, bs_sem, br_sem,
+    ld_sem, in_sem, xs_sem, xr_sem, ys_sem, yr_sem, as_sem, ar_sem, bs_sem, br_sem, near_sem,
 ):
     mark = Marks()
     gx = lax.axis_index("gx")
     yz = lax.axis_index("yz")
 
+    mark("barrier")
+    barrier = pltpu.get_barrier_semaphore()
+    def tell(sem, along, step):
+        here, count = (gx, N_GX) if along == "gx" else (yz, N_YZ)
+        for sign in (1, -1):
+            there = here + sign * step
+
+            @pl.when(there < count if sign > 0 else there >= 0)
+            def _():
+                to = (there, yz) if along == "gx" else (gx, there)
+                pl.semaphore_signal(sem, inc=1, device_id=to, device_id_type=MESH)
+
+    def told(sem, *pairs):
+        total = 0
+        for along, step in pairs:
+            here, count = (gx, N_GX) if along == "gx" else (yz, N_YZ)
+            total = total + (here >= step).astype(jnp.int32) + (here < count - step).astype(jnp.int32)
+        pl.semaphore_wait(sem, total)
+
+    tell(barrier, "gx", 1)
+    tell(barrier, "yz", 1)
     mark("start")
     order = (0, 4, 2, 3, 1)
     small = []
@@ -109,12 +130,48 @@
             )
             c.start()
             loads[f, t] = c
-    mark("barrier")
-    barrier = pltpu.get_barrier_semaphore()
-    for k in range(1, N_GX):
-        pl.semaphore_signal(barrier, inc=1, device_id=(lax.rem(gx + k, N_GX), yz), device_id_type=MESH)
-    for k in range(1, N_YZ):
-        pl.semaphore_signal(barrier, inc=1, device_id=(gx, lax.rem(yz + k, N_YZ)), device_id_type=MESH)
+    mark("barrier_wait")
+    told(barrier, ("gx", 1), ("yz", 1))
+
+    mark("issue")
+    has_left, has_right = gx > 0, gx < N_GX - 1
+    has_low, has_high = yz > 0, yz < N_YZ - 1
+    right, left = (lax.rem(gx + 1, N_GX), yz), (lax.rem(gx + N_GX - 1, N_GX), yz)
+    high, low = (gx, lax.rem(yz + 1, N_YZ)), (gx, lax.rem(yz + N_YZ - 1, N_YZ))
+
+    def xcopy(src, dst, way, k):
+        return pltpu.make_async_remote_copy(
+            src_ref=src, dst_ref=dst, send_sem=xs_sem.at[way, k], recv_sem=xr_sem.at[way, k],
+            device_id=(right, left)[way], device_id_type=MESH,
+        )
+
+    xc = ([], [])
+    for way, plane in ((0, CX - 1), (1, 0)):
+        xc[way].append(xcopy(state.at[:, plane], hal.at[pl.ds(0, 4), 2 + way], way, 0))
+        xc[way].append(xcopy(mean.at[plane], hal.at[4, 2 + way], way, 1))
+        for f in range(5):
+            xc[way].append(xcopy(tsum.at[way, f], hal.at[f, way], way, 2 + f))
+    tell(near_sem.at[0], "gx", 1)
+    tell(near_sem.at[0], "yz", 1)
+    sends = (has_right, has_left)
+    gets = (has_left, has_right)
+    for way in range(2):
+        @pl.when(sends[way])
+        def _():
+            xc[way][0].start()
+            xc[way][1].start()
+
+    yc = ([], [])
+    for k, f in enumerate((0, 2, 4)):
+        for way, (first, there) in enumerate(((8 + CY - 3, 5), (8, 8 + CY))):
+            yc[way].append(pltpu.make_async_remote_copy(
+                src_ref=fld.at[f, :, :, pl.ds(first, 3), :], dst_ref=fld.at[f, :, :, pl.ds(there, 3), :],
+                send_sem=ys_sem.at[way, k], recv_sem=yr_sem.at[way, k],
+                device_id=(high, low)[way], device_id_type=MESH,
+            ))
+    ysends = (has_high, has_low)
+    ygets = (has_low, has_high)
+
     mark("observers")
     to = lax.broadcasted_iota(jnp.int32, (OBS, OBS), 1)
     source = (
@@ -137,68 +194,77 @@
         + jnp.dot(o_mid, perm, preferred_element_type=F32)
         + jnp.dot(o_lo, perm, preferred_element_type=F32)
     )
-    mark("barrier_wait")
-    pl.semaphore_wait(barrier, N_GX + N_YZ - 2)
-
-    mark("issue")
-    has_left, has_right = gx > 0, gx < N_GX - 1
-    has_low, has_high = yz > 0, yz < N_YZ - 1
-    right, left = (lax.rem(gx + 1, N_GX), yz), (lax.rem(gx + N_GX - 1, N_GX), yz)
-    high, low = (gx, lax.rem(yz + 1, N_YZ)), (gx, lax.rem(yz + N_YZ - 1, N_YZ))
-
-    def xcopy(src, dst, way, k):
-        return pltpu.make_async_remote_copy(
-            src_ref=src, dst_ref=dst, send_sem=xs_sem.at[way, k], recv_sem=xr_sem.at[way, k],
-            device_id=(right, left)[way], device_id_type=MESH,
-        )
-
-    xc = ([], [])
-    for way, plane in ((0, CX - 1), (1, 0)):
-        xc[way].append(xcopy(state.at[:, plane], hal.at[pl.ds(0, 4), 2 + way], way, 0))
-        xc[way].append(xcopy(mean.at[plane], hal.at[4, 2 + way], way, 1))
-        for f in range(5):
-            xc[way].append(xcopy(tsum.at[way, f], hal.at[f, way], way, 2 + f))
-    sends = (has_right, has_left)
-    gets = (has_left, has_right)
-    for way in range(2):
-        @pl.when(sends[way])
-        def _():
-            xc[way][0].start()
-            xc[way][1].start()
-
-    yc = ([], [])
-    for k, f in enumerate((0, 2, 4)):
-        for way, (first, there) in enumerate(((8 + CY - 3, 5), (8, 8 + CY))):
-            yc[way].append(pltpu.make_async_remote_copy(
-                src_ref=fld.at[f, :, :, pl.ds(first, 3), :], dst_ref=fld.at[f, :, :, pl.ds(there, 3), :],
-                send_sem=ys_sem.at[way, k], recv_sem=yr_sem.at[way, k],
-                device_id=(high, low)[way], device_id_type=MESH,
-            ))
-    ysends = (has_high, has_low)
-    ygets = (has_low, has_high)
+    mark("columns")
+    for c in small[3:]:
+        c.wait()
+    cell = face_v[...]
+    line = lax.shift_right_logical(cell, 8)
+    fx = lax.shift_right_logical(lax.shift_right_logical(line, 7) * 21846, 16)
+    fy = line - CY * lax.shift_right_logical(lax.shift_right_logical(line, 4) * 21846, 16)
+    fx = fx & (CX - 1)
+    fz = cell & 255
+    rows_v[...] = jnp.zeros((16, 256), F32)
+    rows_v[pl.ds(0, 3), pl.ds(0, FACES_DEV)] = pos_v[...]
+    rows_v[pl.ds(3, 3), pl.ds(0, FACES_DEV)] = normal_v[...]
+    rows_v[pl.ds(6, 1), pl.ds(0, FACES_DEV)] = fx.astype(F32)
+    rows_v[pl.ds(7, 1), pl.ds(0, FACES_DEV)] = fy.astype(F32)
+    rows_v[pl.ds(8, 1), pl.ds(0, FACES_DEV)] = fz.astype(F32)
+    cols = rows_v[...].T
+    col = lambda k: cols[:FACES_DEV, k : k + 1]
+    xcol, ycol, zcol = col(6), col(7), col(8)
+    lane = lax.broadcasted_iota(jnp.int32, (FACES_DEV, 128), 1).astype(F32)
+    zlane = zcol - jnp.where(zcol >= 128.0, 128.0, 0.0)
+    zmask = zlane == lane
+    pick = lambda a: jnp.sum(jnp.where(zmask, a, 0.0), axis=1, keepdims=True)
+    xmask = xcol == lane
+    coef = [
+        jnp.sum(jnp.where(xmask, table_v[pl.ds(k, 1), :], 0.0), axis=1, keepdims=True) for k in range(4)
+    ]
+    upper = lane >= CY
+    hit = jnp.where(upper, lane - CY, lane) == ycol
+    weights = [
+        jnp.where(hit, jnp.where(upper, coef[2 * k + 1], coef[2 * k]), 0.0) for k in range(2)
+    ]
+    mark("geometry")
+    for t in range(4):
+        lanes = slice(128 * t, 128 * t + 128)
+        dx = seen_v[0:1, lanes] - col(0)
+        dy_ = seen_v[1:2, lanes] - col(1)
+        dz_ = seen_v[2:3, lanes] - col(2)
+        inv = lax.rsqrt(dx * dx + dy_ * dy_ + dz_ * dz_)
+        nr = (col(3) * dx + col(4) * dy_ + col(5) * dz_) * inv
+        q1 = INV_FOUR_PI * inv
+        geo[0, :, lanes] = q1
+        geo[1, :, lanes] = q1 * nr
+        geo[2, :, lanes] = q1 * nr * inv
+
+    mark("wait_load")
+    for f in order[:3]:
+        loads[f, 0].wait()
+        loads[f, 1].wait()
+        for way in range(2):
+            @pl.when(ysends[way])
+            def _():
+                yc[way][f // 2].start()
 
     mark("sweeps")
     small[2].wait()
 
     def along_z(j):
-        q = j // 4
-        x0 = 8 * (j - 4 * q)
+        q = j // 2
+        x0 = 16 * (j - 2 * q)
         f = jnp.where(q == 0, 0, 5 - q)
-        v = fld[f, pl.ds(x0, 8), :, pl.ds(8, CY), :]
-        v = jnp.concatenate([v[:, 0], v[:, 1]], axis=-1).reshape(8 * CY, NZ)
+        v = fld[f, pl.ds(x0, 16), :, pl.ds(8, CY), :]
+        v = jnp.concatenate([v[:, 0], v[:, 1]], axis=-1).reshape(16 * CY, NZ)
         hi, lo = split2(v)
         out = jnp.dot(jnp.concatenate([hi, lo, hi], axis=1), dz_v[...], preferred_element_type=F32)
-        zed[q, pl.ds(x0, 8)] = out.reshape(8, CY, NZ)
+        zed[q, pl.ds(x0, 16)] = out.reshape(16, CY, NZ)
 
     jobs = 0
-    for f, per_half in zip(order, (1, 1, 1, 2, 1)):
-        loads[f, 0].wait()
-        loads[f, 1].wait()
-        if f in (0, 2, 4):
-            for way in range(2):
-                @pl.when(ysends[way])
-                def _():
-                    yc[way][f // 2].start()
+    for f, per_half in zip(order, (1, 1, 0, 1, 0)):
+        if f not in (0, 2, 4):
+            loads[f, 0].wait()
+            loads[f, 1].wait()
 
         def sweep(t, _, f=f, per_half=per_half, jobs=jobs):
             zero = jnp.zeros((CY, 128), F32)
@@ -231,6 +297,9 @@
             def _():
                 xc[way][2 + f].start()
 
+    told(near_sem.at[0], ("gx", 1), ("yz", 1))
+    tell(near_sem.at[1], "yz", 2)
+    tell(near_sem.at[2], "gx", 2)
     mark("ends")
     for way, there in ((0, jnp.logical_not(has_left)), (1, jnp.logical_not(has_right))):
         @pl.when(there)
@@ -256,8 +325,6 @@
                 fld[f, :, :, pl.ds(row, 3), :] = jnp.zeros((CX, 2, 3, 128), F32)
 
     mark("wait_y")
-    for c in small[3:]:
-        c.wait()
     for way in range(2):
         @pl.when(ygets[way])
         def _():
@@ -309,74 +376,55 @@
 
     lax.fori_loop(0, FACES_DEV // 8, gather, 0)
 
-    mark("columns")
-    cell = face_v[...]
-    line = lax.shift_right_logical(cell, 8)
-    fx = lax.shift_right_logical(lax.shift_right_logical(line, 7) * 21846, 16)
-    fy = line - CY * lax.shift_right_logical(lax.shift_right_logical(line, 4) * 21846, 16)
-    fx = fx & (CX - 1)
-    fz = cell & 255
-    rows_v[...] = jnp.zeros((16, 256), F32)
-    rows_v[pl.ds(0, 3), pl.ds(0, FACES_DEV)] = pos_v[...]
-    rows_v[pl.ds(3, 3), pl.ds(0, FACES_DEV)] = normal_v[...]
-    rows_v[pl.ds(6, 1), pl.ds(0, FACES_DEV)] = fx.astype(F32)
-    rows_v[pl.ds(7, 1), pl.ds(0, FACES_DEV)] = fy.astype(F32)
-    rows_v[pl.ds(8, 1), pl.ds(0, FACES_DEV)] = fz.astype(F32)
-    cols = rows_v[...].T
-    col = lambda k: cols[:FACES_DEV, k : k + 1]
-    xcol, ycol, zcol = col(6), col(7), col(8)
-    lane = lax.broadcasted_iota(jnp.int32, (FACES_DEV, 128), 1).astype(F32)
-    zlane = zcol - jnp.where(zcol >= 128.0, 128.0, 0.0)
-    zmask = zlane == lane
-    pick = lambda a: jnp.sum(jnp.where(zmask, a, 0.0), axis=1, keepdims=True)
+    told(near_sem.at[1], ("yz", 2))
+    tell(near_sem.at[3], "yz", 4)
+    mark("picks")
     face0 = [pick(stg[q]) for q in range(7)]
-    xmask = xcol == lane
-    coef = [
-        jnp.sum(jnp.where(xmask, table_v[pl.ds(k, 1), :], 0.0), axis=1, keepdims=True) for k in range(4)
-    ]
-    wide = lax.broadcasted_iota(jnp.int32, (FACES_DEV, 4 * CY), 1)
-    part = (wide >= CY).astype(jnp.int32) + (wide >= 2 * CY).astype(jnp.int32) + (wide >= 3 * CY).astype(jnp.int32)
-    hit = (wide - CY * part).astype(F32) == ycol
-    weight = jnp.where(
-        hit,
-        jnp.where(part == 0, coef[0], jnp.where(part == 1, coef[1], jnp.where(part == 2, coef[2], coef[3]))),
-        0.0,
-    )
-    hi, lo = split2(weight)
-    weight = jnp.concatenate([hi, lo, hi], axis=1)
-
-    mark("geometry")
-    for t in range(4):
-        lanes = slice(128 * t, 128 * t + 128)
-        dx = seen_v[0:1, lanes] - col(0)
-        dy_ = seen_v[1:2, lanes] - col(1)
-        dz_ = seen_v[2:3, lanes] - col(2)
-        inv = lax.rsqrt(dx * dx + dy_ * dy_ + dz_ * dz_)
-        nr = (col(3) * dx + col(4) * dy_ + col(5) * dz_) * inv
-        q1 = INV_FOUR_PI * inv
-        geo[0, :, lanes] = q1
-        geo[1, :, lanes] = q1 * nr
-        geo[2, :, lanes] = q1 * nr * inv
+    fp, fu, fm = face0[4], face0[5], face0[6]
+    fn = [col(3 + k) for k in range(3)]
+    to0 = (fm, jnp.ones_like(fm))
+    toa = (fn[0], fn[0] * fm, fn[1] * fm, fn[2] * fm, fn[0] * fu)
+
+    def left_of(k, scales):
+        out = []
+        for scale in scales:
+            hi, lo = split2(weights[k] * scale)
+            out += [hi, lo, hi]
+        return jnp.concatenate(out, axis=1)
+
+    lefts = [(left_of(k, to0), left_of(k, toa)) for k in range(2)]
 
     mark("wait_x")
     for way in range(2):
         @pl.when(gets[way])
         def _():
-            for c in xc[way]:
+            xc[way][0].wait_recv()
+            xc[way][1].wait_recv()
+
+    zwide = lax.broadcasted_iota(jnp.int32, (FACES_DEV, NZ), 1).astype(F32) == zcol
+    pad = jnp.zeros((128 - 2 * CY, NZ), BF16)
+
+    def at_faces(k):
+        right = []
+        for f in range(5):
+            hi, lo = split2(hal[f, pl.ds(2 * k, 2)].reshape(2 * CY, NZ))
+            right += [hi, pad, hi, pad, lo, pad]
+        return [
+            jnp.dot(a, jnp.concatenate(right[: 6 * n], axis=0), preferred_element_type=F32)
+            for a, n in zip(lefts[k], (2, 5))
+        ]
+
+    edge0, edgea = at_faces(1)
+    mark("wait_t")
+    for way in range(2):
+        @pl.when(gets[way])
+        def _():
+            for c in xc[way][2:]:
                 c.wait_recv()
     mark("near")
-    near = []
-    for f in range(5):
-        hi, lo = split2(hal[f].reshape(4 * CY, NZ))
-        near.append(jnp.dot(weight, jnp.concatenate([hi, hi, lo], axis=0), preferred_element_type=F32))
-    fp, fu, fm = face0[4], face0[5], face0[6]
-    add0 = fm * near[0] + near[1]
-    adda = (
-        col(3) * (fm * near[1] + fu * near[4] + near[0])
-        + (col(4) * fm) * near[2] + (col(5) * fm) * near[3]
-    )
-    zwide = lax.broadcasted_iota(jnp.int32, (FACES_DEV, NZ), 1).astype(F32) == zcol
+    add0, adda = at_faces(0)
     pickw = lambda a: jnp.sum(jnp.where(zwide, a, 0.0), axis=1, keepdims=True)
+    add0, adda = add0 + edge0, adda + edgea
     rate0 = -(face0[0] + pickw(add0))
     ratea = -(col(3) * face0[1] + col(4) * face0[2] + col(5) * face0[3] + pickw(adda))
     pnext = fp + TIME_STEP * rate0
@@ -384,7 +432,6 @@
         lanes = slice(128 * t, 128 * t + 128)
         geo[0, :, lanes] = ratea * geo[0, :, lanes] + rate0 * geo[1, :, lanes] + pnext * geo[2, :, lanes]
 
-    mark("bins")
     def patterns(n, _):
         t = n // 8
         block = n - 8 * t
@@ -405,28 +452,33 @@
             binned[t, pl.ds(pl.multiple_of(64 * block, 8) + 8 * k, 8), :] = acc[k]
         return 0
 
-    lax.fori_loop(0, 32, patterns, 0)
-    mark("pack")
-
     def folded(t):
         out = binned[t, pl.ds(0, BINS, stride=8), :]
         for k in range(1, 8):
             out = out + binned[t, pl.ds(k, BINS, stride=8), :]
         return out
 
+    mark("near_wait")
+    told(near_sem.at[2], ("gx", 2))
+    tell(near_sem.at[4], "gx", 4)
+    mark("bins")
+    lax.fori_loop(0, 32, patterns, 0, unroll=2)
+    mark("pack")
+    had = had_v[...]
     for t in range(2):
         both = jnp.concatenate([folded(t), folded(2 + t)], axis=0).T
         hi = both.astype(BF16)
         rest = both - hi.astype(F32)
         mid = rest.astype(BF16)
         lo = (rest - mid.astype(F32)).astype(BF16)
-        had = had_v[...]
         packed[pl.ds(128 * t, 128), :] = (
             jnp.dot(hi, had, preferred_element_type=F32)
             + jnp.dot(mid, had, preferred_element_type=F32)
             + jnp.dot(lo, had, preferred_element_type=F32)
         )
-
+    told(near_sem.at[4], ("gx", 4))
+    tell(near_sem.at[5], "gx", 8)
+    told(near_sem.at[3], ("yz", 4))
     ac = []
     for k in range(1, N_YZ):
         peer = lax.rem(yz + k, N_YZ)
@@ -473,6 +525,8 @@
         total = total + recv_a[k]
     for g in range(N_GX):
         send_b[g] = total[2 * g : 2 * g + 2]
+    mark("far_wait")
+    told(near_sem.at[5], ("gx", 8))
     bc = []
     for k in range(1, N_GX):
         peer = lax.rem(gx + k, N_GX)
@@ -560,13 +614,13 @@
             vm((8, OBS), F32),
             vm((4, 8 * BINS, 128), F32),
             vm((256, 128), F32),
-            vm((N_YZ - 1, 32, 128), F32),
+            vm((N_YZ, 32, 128), F32),
             vm((N_GX, 2, 128), F32),
             vm((N_GX - 1, 2, 128), F32),
             pltpu.SMEM((4, 128), F32),
             pltpu.SMEM((1, FACES_DEV), jnp.int32),
             dma((5, 2)), dma((10,)), dma((2, 7)), dma((2, 7)), dma((2, 3)), dma((2, 3)),
-            dma((N_YZ - 1,)), dma((N_YZ - 1,)), dma((N_GX - 1,)), dma((N_GX - 1,)),
+            dma((N_YZ,)), dma((N_YZ,)), dma((N_GX - 1,)), dma((N_GX - 1,)), pltpu.SemaphoreType.REGULAR((6,)),
         ],
         compiler_params=pltpu.CompilerParams(
             collective_id=0, has_side_effects=True, vmem_limit_bytes=57 * 2**20 + 2**19
@@ -575,7 +629,26 @@
         state, mean_flow, face_cell.reshape(1, FACES_DEV), face_normal, face_pos, observer_pos, time_bin,
         dz, jnp.asarray(table), jnp.asarray(table[:4]), jnp.asarray(had, BF16),
     )
-    return nxt, sig
+
+    def write_out(nxt_ref, sig_ref, nxt_out, sig_out, sem):
+        copies = [pltpu.make_async_copy(sig_ref, sig_out, sem.at[4])]
+        copies += [pltpu.make_async_copy(nxt_ref.at[k], nxt_out.at[k], sem.at[k]) for k in range(4)]
+        for c in copies:
+            c.start()
+        for c in copies:
+            c.wait()
+
+    return pl.pallas_call(
+        write_out,
+        out_shape=(
+            jax.ShapeDtypeStruct((4, CX, CY, NZ), F32),
+            jax.ShapeDtypeStruct((4, BINS), F32),
+        ),
+        in_specs=[pl.BlockSpec(memory_space=pltpu.VMEM)] * 2,
+        out_specs=(anywhere, anywhere),
+        scratch_shapes=[dma((5,))],
+        compiler_params=pltpu.CompilerParams(vmem_limit_bytes=2**20),
+    )(pltpu.with_memory_space_constraint(nxt, pltpu.VMEM), pltpu.with_memory_space_constraint(sig, pltpu.VMEM))
 
 
 def solution(mesh):

time: 38.2 us -> 36.8 us (0.963)
  local copies, waits for them, and re-layouts: 3.28 us -> 0 us
  Pallas kernels: 33.8 us -> 35.7 us
    unnamed x2 -> x0, local copies, waits for them, and re-layouts: 3.28 us -> none
    pallas_call x0 -> x1, Pallas kernels: none -> 2.74 us  [per_device(): pl.pallas_call(write_out, out_shape=(jax.ShapeDtypeStruct((4, CX, CY, NZ)...]
    pallas_call x1, Pallas kernels: 33.8 us -> 33 us  [per_device(): pl.pallas_call(functools.partial(kernel, ends), out_shape=(vm((4, CX, CY,...]
where the time goes in v3:
time: 36.8 us; the launch traced here: 36.4 us
  Pallas kernels  35.7 us (97%)
  between operations  0.64 us (2%)
    pallas_call x1, Pallas kernels, per_device(): pl.pallas_call(functools.partial(kernel, ends), out_shape=(vm((4, CX, CY,...  33 us
    pallas_call x1, Pallas kernels, per_device(): pl.pallas_call(write_out, out_shape=(jax.ShapeDtypeStruct((4, CX, CY, NZ)...  2.74 us

profile of v3, /device:TPU:0, one launch (start us, length us, event | category | flops | bytes accessed | tf_op | source)
XLA Modules:
  0.0 36.4 jit_solution(8005362354145689522)
XLA Ops:
  0.6 33.0 %shard_map.122 = (f32[4,32,48,256]{3,2,1,0:T(8,128)S(1)}, f32[4,64]{1,0:T(4,128)S(1)}) custom-call(f32[4,32,48,256]{3,2,1,0:T(8,128)} %state.1, f32[32,48,256]{2,1,0:T(8,128)} %mean.1, s32[1,192]{1,0:T(1,128)} %bitcast.1, f32[3,192]{1,0:T(4,128)} %normal.1, f32[3,192]{1,0:T(4,128)} %pos.1, f32[3,512]{1,0:T(4,128)} %obs.1, s32[192,512]{1,0:T(8,128)} %tbin.1, ...), custom_call_target="tpu_custom_call" | custom-call | tf_op jit(solution)/shard_map/pallas_call | solution.py:588
  33.6 2.7 %shard_map.123 = (f32[4,32,48,256]{3,2,1,0:T(8,128)}, f32[4,64]{1,0:T(4,128)}) custom-call(f32[4,32,48,256]{3,2,1,0:T(8,128)S(1)} %get-tuple-element.4.nxt_ref, f32[4,64]{1,0:T(4,128)S(1)} %get-tuple-element.5.sig_ref), custom_call_target="tpu_custom_call" | custom-call | tf_op jit(solution)/shard_map/pallas_call | solution.py:641

commit v4 on v3

--- a/solution.py
+++ b/solution.py
@@ -145,12 +145,16 @@
             device_id=(right, left)[way], device_id_type=MESH,
         )
 
-    xc = ([], [])
+    planes, sums = ([], []), ([], [])
     for way, plane in ((0, CX - 1), (1, 0)):
-        xc[way].append(xcopy(state.at[:, plane], hal.at[pl.ds(0, 4), 2 + way], way, 0))
-        xc[way].append(xcopy(mean.at[plane], hal.at[4, 2 + way], way, 1))
+        planes[way].append(xcopy(state.at[:, plane], hal.at[pl.ds(0, 4), 2 + way], way, 0))
+        planes[way].append(xcopy(mean.at[plane], hal.at[4, 2 + way], way, 0))
         for f in range(5):
-            xc[way].append(xcopy(tsum.at[way, f], hal.at[f, way], way, 2 + f))
+            sums[way].append(xcopy(tsum.at[way, f], hal.at[f, way], way, 1 + f // 4))
+    all_planes = [xcopy(tsum.at[way], hal.at[:, 2 + way], way, 0) for way in range(2)]
+    all_sums = [
+        (xcopy(tsum.at[way, pl.ds(0, 4)], hal.at[pl.ds(0, 4), way], way, 1), sums[way][4]) for way in range(2)
+    ]
     tell(near_sem.at[0], "gx", 1)
     tell(near_sem.at[0], "yz", 1)
     sends = (has_right, has_left)
@@ -158,8 +162,8 @@
     for way in range(2):
         @pl.when(sends[way])
         def _():
-            xc[way][0].start()
-            xc[way][1].start()
+            planes[way][0].start()
+            planes[way][1].start()
 
     yc = ([], [])
     for k, f in enumerate((0, 2, 4)):
@@ -175,8 +179,8 @@
     mark("observers")
     to = lax.broadcasted_iota(jnp.int32, (OBS, OBS), 1)
     source = (
-        32 * (lax.shift_right_logical(to, 1) & 15) + 4 * (lax.shift_right_logical(to, 5) & 7)
-        + 2 * (to & 1) + lax.shift_right_logical(to, 8)
+        32 * (to & 15) + 4 * (lax.shift_right_logical(to, 4) & 7)
+        + 2 * lax.shift_right_logical(to, 8) + (lax.shift_right_logical(to, 7) & 1)
     )
     perm = jnp.where(lax.broadcasted_iota(jnp.int32, (OBS, OBS), 0) == source, 1.0, 0.0).astype(BF16)
     small[0].wait()
@@ -253,7 +257,7 @@
     def along_z(j):
         q = j // 2
         x0 = 16 * (j - 2 * q)
-        f = jnp.where(q == 0, 0, 5 - q)
+        f = jnp.where(q == 0, 0, q + 2)
         v = fld[f, pl.ds(x0, 16), :, pl.ds(8, CY), :]
         v = jnp.concatenate([v[:, 0], v[:, 1]], axis=-1).reshape(16 * CY, NZ)
         hi, lo = split2(v)
@@ -261,7 +265,7 @@
         zed[q, pl.ds(x0, 16)] = out.reshape(16, CY, NZ)
 
     jobs = 0
-    for f, per_half in zip(order, (1, 1, 0, 1, 0)):
+    for f, per_half in zip((0, 3, 2, 1, 4), (1, 1, 1, 0, 0)):
         if f not in (0, 2, 4):
             loads[f, 0].wait()
             loads[f, 1].wait()
@@ -291,15 +295,16 @@
             return 0
 
         lax.fori_loop(0, 2, sweep, 0)
+        if f == 0:
+            told(near_sem.at[0], ("gx", 1), ("yz", 1))
+            tell(near_sem.at[1], "yz", 2)
+            tell(near_sem.at[2], "gx", 2)
         jobs += 2 * per_half
         for way in range(2):
             @pl.when(sends[way])
             def _():
-                xc[way][2 + f].start()
-
-    told(near_sem.at[0], ("gx", 1), ("yz", 1))
-    tell(near_sem.at[1], "yz", 2)
-    tell(near_sem.at[2], "gx", 2)
+                sums[way][f].start()
+
     mark("ends")
     for way, there in ((0, jnp.logical_not(has_left)), (1, jnp.logical_not(has_right))):
         @pl.when(there)
@@ -337,7 +342,7 @@
             for t in range(2):
                 x = 2 * n + j
                 at = lambda f, s=0: fld[f, x, t, pl.ds(8 + s, CY), :]
-                pz, mz, wz = (zed[q, x, :, 128 * t : 128 * t + 128] for q in range(3))
+                pz, wz, mz = (zed[q, x, :, 128 * t : 128 * t + 128] for q in range(3))
 
                 def dy(f):
                     return (
@@ -378,6 +383,8 @@
 
     told(near_sem.at[1], ("yz", 2))
     tell(near_sem.at[3], "yz", 4)
+    told(near_sem.at[2], ("gx", 2))
+    tell(near_sem.at[4], "gx", 4)
     mark("picks")
     face0 = [pick(stg[q]) for q in range(7)]
     fp, fu, fm = face0[4], face0[5], face0[6]
@@ -392,39 +399,48 @@
             out += [hi, lo, hi]
         return jnp.concatenate(out, axis=1)
 
-    lefts = [(left_of(k, to0), left_of(k, toa)) for k in range(2)]
+    lefts = [(left_of(k, to0), left_of(k, toa[:4]), left_of(k, toa[4:])) for k in range(2)]
 
     mark("wait_x")
     for way in range(2):
         @pl.when(gets[way])
         def _():
-            xc[way][0].wait_recv()
-            xc[way][1].wait_recv()
+            all_planes[way].wait_recv()
 
     zwide = lax.broadcasted_iota(jnp.int32, (FACES_DEV, NZ), 1).astype(F32) == zcol
     pad = jnp.zeros((128 - 2 * CY, NZ), BF16)
 
-    def at_faces(k):
-        right = []
-        for f in range(5):
+    def rights(k, fields):
+        out = []
+        for f in fields:
             hi, lo = split2(hal[f, pl.ds(2 * k, 2)].reshape(2 * CY, NZ))
-            right += [hi, pad, hi, pad, lo, pad]
-        return [
-            jnp.dot(a, jnp.concatenate(right[: 6 * n], axis=0), preferred_element_type=F32)
-            for a, n in zip(lefts[k], (2, 5))
-        ]
-
-    edge0, edgea = at_faces(1)
+            out += [hi, pad, hi, pad, lo, pad]
+        return out
+
+    def times(a, right):
+        return jnp.dot(a, jnp.concatenate(right, axis=0), preferred_element_type=F32)
+
+    def most_at_faces(k):
+        right = rights(k, range(4))
+        return times(lefts[k][0], right[:12]), times(lefts[k][1], right)
+
+    add0, adda = most_at_faces(1)
+    adda = adda + times(lefts[1][2], rights(1, (4,)))
     mark("wait_t")
     for way in range(2):
         @pl.when(gets[way])
         def _():
-            for c in xc[way][2:]:
-                c.wait_recv()
+            all_sums[way][0].wait_recv()
+    more0, morea = most_at_faces(0)
+    add0, adda = add0 + more0, adda + morea
+    mark("wait_u")
+    for way in range(2):
+        @pl.when(gets[way])
+        def _():
+            all_sums[way][1].wait_recv()
     mark("near")
-    add0, adda = at_faces(0)
+    adda = adda + times(lefts[0][2], rights(0, (4,)))
     pickw = lambda a: jnp.sum(jnp.where(zwide, a, 0.0), axis=1, keepdims=True)
-    add0, adda = add0 + edge0, adda + edgea
     rate0 = -(face0[0] + pickw(add0))
     ratea = -(col(3) * face0[1] + col(4) * face0[2] + col(5) * face0[3] + pickw(adda))
     pnext = fp + TIME_STEP * rate0
@@ -459,35 +475,48 @@
         return out
 
     mark("near_wait")
-    told(near_sem.at[2], ("gx", 2))
-    tell(near_sem.at[4], "gx", 4)
-    mark("bins")
-    lax.fori_loop(0, 32, patterns, 0, unroll=2)
-    mark("pack")
-    had = had_v[...]
-    for t in range(2):
-        both = jnp.concatenate([folded(t), folded(2 + t)], axis=0).T
+    told(near_sem.at[4], ("gx", 4))
+    tell(near_sem.at[5], "gx", 8)
+    def acopy(half, k):
+        peer = lax.rem(yz + k, N_YZ)
+        return pltpu.make_async_remote_copy(
+            src_ref=packed.at[half, pl.ds(pl.multiple_of(16 * peer, 16), 16), :], dst_ref=recv_a.at[half, k - 1],
+            send_sem=as_sem.at[half], recv_sem=ar_sem.at[half], device_id=(gx, peer), device_id_type=MESH,
+        )
+
+    def bcopy(k):
+        peer = lax.rem(gx + k, N_GX)
+        return pltpu.make_async_remote_copy(
+            src_ref=send_b.at[peer], dst_ref=recv_b.at[k - 1],
+            send_sem=bs_sem, recv_sem=br_sem, device_id=(peer, yz), device_id_type=MESH,
+        )
+
+    def whole(ref, send_sem, recv_sem, to):
+        return pltpu.make_async_remote_copy(
+            src_ref=ref, dst_ref=ref, send_sem=send_sem, recv_sem=recv_sem, device_id=to, device_id_type=MESH,
+        )
+
+    awhole = [whole(recv_a.at[half], as_sem.at[half], ar_sem.at[half], high) for half in range(2)]
+    bwhole = whole(recv_b, bs_sem, br_sem, right)
+
+    told(near_sem.at[3], ("yz", 4))
+    for half in range(2):
+        mark(f"bins{half}")
+        lax.fori_loop(16 * half, 16 * half + 16, patterns, 0, unroll=2)
+        mark(f"pack{half}")
+        had = had_v[...]
+        both = jnp.concatenate([folded(2 * half), folded(2 * half + 1)], axis=0).T
         hi = both.astype(BF16)
         rest = both - hi.astype(F32)
         mid = rest.astype(BF16)
         lo = (rest - mid.astype(F32)).astype(BF16)
-        packed[pl.ds(128 * t, 128), :] = (
+        packed[half] = (
             jnp.dot(hi, had, preferred_element_type=F32)
             + jnp.dot(mid, had, preferred_element_type=F32)
             + jnp.dot(lo, had, preferred_element_type=F32)
         )
-    told(near_sem.at[4], ("gx", 4))
-    tell(near_sem.at[5], "gx", 8)
-    told(near_sem.at[3], ("yz", 4))
-    ac = []
-    for k in range(1, N_YZ):
-        peer = lax.rem(yz + k, N_YZ)
-        c = pltpu.make_async_remote_copy(
-            src_ref=packed.at[pl.ds(pl.multiple_of(32 * peer, 32), 32), :], dst_ref=recv_a.at[k - 1],
-            send_sem=as_sem.at[k - 1], recv_sem=ar_sem.at[k - 1], device_id=(gx, peer), device_id_type=MESH,
-        )
-        c.start()
-        ac.append(c)
+        for k in (4, 3, 5, 2, 6, 1, 7):
+            acopy(half, k).start()
 
     mark("finish_a")
     def finish(x, _):
@@ -519,32 +548,27 @@
     lax.fori_loop(0, CX // 2, finish, 0)
 
     mark("wait_a")
-    total = packed[pl.ds(pl.multiple_of(32 * yz, 32), 32), :]
-    for k in range(N_YZ - 1):
-        ac[k].wait_recv()
-        total = total + recv_a[k]
-    for g in range(N_GX):
-        send_b[g] = total[2 * g : 2 * g + 2]
+    for half in range(2):
+        awhole[half].wait_recv()
+        total = packed[half, pl.ds(pl.multiple_of(16 * yz, 16), 16), :]
+        for k in range(N_YZ - 1):
+            total = total + recv_a[half, k]
+        for g in range(N_GX):
+            send_b[g, pl.ds(half, 1), :] = total[g : g + 1]
     mark("far_wait")
     told(near_sem.at[5], ("gx", 8))
-    bc = []
-    for k in range(1, N_GX):
-        peer = lax.rem(gx + k, N_GX)
-        c = pltpu.make_async_remote_copy(
-            src_ref=send_b.at[peer], dst_ref=recv_b.at[k - 1],
-            send_sem=bs_sem.at[k - 1], recv_sem=br_sem.at[k - 1], device_id=(peer, yz), device_id_type=MESH,
-        )
-        c.start()
-        bc.append(c)
+    hops = lambda k: min(k // 4, 4 - k // 4) + min(k % 4, 4 - k % 4)
+    for k in sorted(range(1, N_GX), key=hops, reverse=True):
+        bcopy(k).start()
 
     mark("finish_b")
     lax.fori_loop(CX // 2, CX, finish, 0)
     edges()
 
     mark("wait_b")
+    bwhole.wait_recv()
     total = send_b[gx]
     for k in range(N_GX - 1):
-        bc[k].wait_recv()
         total = total + recv_b[k]
     for h in range(2):
         for h2 in range(2):
@@ -554,14 +578,14 @@
     for way in range(2):
         @pl.when(sends[way])
         def _():
-            for c in xc[way]:
+            for c in (all_planes[way], *all_sums[way]):
                 c.wait_send()
 
         @pl.when(ysends[way])
         def _():
             for c in yc[way]:
                 c.wait_send()
-    for c in ac + bc:
+    for c in (*awhole, bwhole):
         c.wait_send()
     mark(None)
 
@@ -613,14 +637,14 @@
             vm((16, 256), F32),
             vm((8, OBS), F32),
             vm((4, 8 * BINS, 128), F32),
-            vm((256, 128), F32),
-            vm((N_YZ, 32, 128), F32),
+            vm((2, 128, 128), F32),
+            vm((2, N_YZ - 1, 16, 128), F32),
             vm((N_GX, 2, 128), F32),
             vm((N_GX - 1, 2, 128), F32),
             pltpu.SMEM((4, 128), F32),
             pltpu.SMEM((1, FACES_DEV), jnp.int32),
-            dma((5, 2)), dma((10,)), dma((2, 7)), dma((2, 7)), dma((2, 3)), dma((2, 3)),
-            dma((N_YZ,)), dma((N_YZ,)), dma((N_GX - 1,)), dma((N_GX - 1,)), pltpu.SemaphoreType.REGULAR((6,)),
+            dma((5, 2)), dma((10,)), dma((2, 3)), dma((2, 3)), dma((2, 3)), dma((2, 3)),
+            dma((2,)), dma((2,)), dma(()), dma(()), pltpu.SemaphoreType.REGULAR((6,)),
         ],
         compiler_params=pltpu.CompilerParams(
             collective_id=0, has_side_effects=True, vmem_limit_bytes=57 * 2**20 + 2**19

time: 36.8 us -> 35.8 us (0.973)
  Pallas kernels: 35.7 us -> 34.7 us
    pallas_call x1, Pallas kernels: 33 us -> 31.9 us  [per_device(): pl.pallas_call(functools.partial(kernel, ends), out_shape=(vm((4, CX, CY,...]
where the time goes in v4:
time: 35.8 us; the launch traced here: 35.3 us
  Pallas kernels  34.7 us (97%)
  between operations  0.64 us (2%)
    pallas_call x1, Pallas kernels, per_device(): pl.pallas_call(functools.partial(kernel, ends), out_shape=(vm((4, CX, CY,...  31.9 us
    pallas_call x1, Pallas kernels, per_device(): pl.pallas_call(write_out, out_shape=(jax.ShapeDtypeStruct((4, CX, CY, NZ)...  2.74 us

profile of v4, /device:TPU:0, one launch (start us, length us, event | category | flops | bytes accessed | tf_op | source)
XLA Modules:
  0.0 35.3 jit_solution(3658122968856204200)
XLA Ops:
  0.6 31.9 %shard_map.122 = (f32[4,32,48,256]{3,2,1,0:T(8,128)S(1)}, f32[4,64]{1,0:T(4,128)S(1)}) custom-call(f32[4,32,48,256]{3,2,1,0:T(8,128)} %state.1, f32[32,48,256]{2,1,0:T(8,128)} %mean.1, s32[1,192]{1,0:T(1,128)} %bitcast.1, f32[3,192]{1,0:T(4,128)} %normal.1, f32[3,192]{1,0:T(4,128)} %pos.1, f32[3,512]{1,0:T(4,128)} %obs.1, s32[192,512]{1,0:T(8,128)} %tbin.1, ...), custom_call_target="tpu_custom_call" | custom-call | tf_op jit(solution)/shard_map/pallas_call | solution.py:612
  32.6 2.7 %shard_map.123 = (f32[4,32,48,256]{3,2,1,0:T(8,128)}, f32[4,64]{1,0:T(4,128)}) custom-call(f32[4,32,48,256]{3,2,1,0:T(8,128)S(1)} %get-tuple-element.4.nxt_ref, f32[4,64]{1,0:T(4,128)S(1)} %get-tuple-element.5.sig_ref), custom_call_target="tpu_custom_call" | custom-call | tf_op jit(solution)/shard_map/pallas_call | solution.py:665

commit v5 on v4

--- a/solution.py
+++ b/solution.py
@@ -165,16 +165,32 @@
             planes[way][0].start()
             planes[way][1].start()
 
+
     yc = ([], [])
     for k, f in enumerate((0, 2, 4)):
         for way, (first, there) in enumerate(((8 + CY - 3, 5), (8, 8 + CY))):
             yc[way].append(pltpu.make_async_remote_copy(
                 src_ref=fld.at[f, :, :, pl.ds(first, 3), :], dst_ref=fld.at[f, :, :, pl.ds(there, 3), :],
-                send_sem=ys_sem.at[way, k], recv_sem=yr_sem.at[way, k],
+                send_sem=ys_sem.at[way], recv_sem=yr_sem.at[way],
                 device_id=(high, low)[way], device_id_type=MESH,
             ))
+    yall = [
+        pltpu.make_async_remote_copy(
+            src_ref=fld.at[pl.ds(0, 3), :, :, pl.ds(row, 3), :], dst_ref=fld.at[pl.ds(0, 3), :, :, pl.ds(row, 3), :],
+            send_sem=ys_sem.at[way], recv_sem=yr_sem.at[way], device_id=(high, low)[way], device_id_type=MESH,
+        )
+        for way, row in ((0, 5), (1, 8 + CY))
+    ]
     ysends = (has_high, has_low)
     ygets = (has_low, has_high)
+
+    def send_y(f):
+        loads[f, 0].wait()
+        loads[f, 1].wait()
+        for way in range(2):
+            @pl.when(ysends[way])
+            def _():
+                yc[way][f // 2].start()
 
     mark("observers")
     to = lax.broadcasted_iota(jnp.int32, (OBS, OBS), 1)
@@ -198,6 +214,7 @@
         + jnp.dot(o_mid, perm, preferred_element_type=F32)
         + jnp.dot(o_lo, perm, preferred_element_type=F32)
     )
+    send_y(0)
     mark("columns")
     for c in small[3:]:
         c.wait()
@@ -229,6 +246,7 @@
     weights = [
         jnp.where(hit, jnp.where(upper, coef[2 * k + 1], coef[2 * k]), 0.0) for k in range(2)
     ]
+    send_y(4)
     mark("geometry")
     for t in range(4):
         lanes = slice(128 * t, 128 * t + 128)
@@ -242,15 +260,7 @@
         geo[1, :, lanes] = q1 * nr
         geo[2, :, lanes] = q1 * nr * inv
 
-    mark("wait_load")
-    for f in order[:3]:
-        loads[f, 0].wait()
-        loads[f, 1].wait()
-        for way in range(2):
-            @pl.when(ysends[way])
-            def _():
-                yc[way][f // 2].start()
-
+    send_y(2)
     mark("sweeps")
     small[2].wait()
 
@@ -333,8 +343,7 @@
     for way in range(2):
         @pl.when(ygets[way])
         def _():
-            for k in range(3):
-                yc[way][k].wait_recv()
+            yall[way].wait_recv()
 
     mark("local")
     def local(n, _):
@@ -459,11 +468,11 @@
             rows = pl.ds(8 * g, 8)
             what = geo[0, rows, lanes]
             geo[0, rows, lanes] = what * sgn[bit, rows, lanes]
-            low = [sgn[k, rows, lanes] for k in range(3)]
-            for k in range(8):
-                if k:
-                    what = what * low[0 if k % 2 else (1 if k % 4 else 2)]
-                acc[k] = acc[k] + what
+            parts = [what]
+            for k in range(3):
+                sign = sgn[k, rows, lanes]
+                parts += [part * sign for part in parts]
+            acc = [a + part for a, part in zip(acc, parts)]
         for k in range(8):
             binned[t, pl.ds(pl.multiple_of(64 * block, 8) + 8 * k, 8), :] = acc[k]
         return 0
@@ -474,9 +483,6 @@
             out = out + binned[t, pl.ds(k, BINS, stride=8), :]
         return out
 
-    mark("near_wait")
-    told(near_sem.at[4], ("gx", 4))
-    tell(near_sem.at[5], "gx", 8)
     def acopy(half, k):
         peer = lax.rem(yz + k, N_YZ)
         return pltpu.make_async_remote_copy(
@@ -502,7 +508,7 @@
     told(near_sem.at[3], ("yz", 4))
     for half in range(2):
         mark(f"bins{half}")
-        lax.fori_loop(16 * half, 16 * half + 16, patterns, 0, unroll=2)
+        lax.fori_loop(16 * half, 16 * half + 16, patterns, 0, unroll=4)
         mark(f"pack{half}")
         had = had_v[...]
         both = jnp.concatenate([folded(2 * half), folded(2 * half + 1)], axis=0).T
@@ -517,6 +523,9 @@
         )
         for k in (4, 3, 5, 2, 6, 1, 7):
             acopy(half, k).start()
+        if half == 0:
+            told(near_sem.at[4], ("gx", 4))
+            tell(near_sem.at[5], "gx", 8)
 
     mark("finish_a")
     def finish(x, _):
@@ -583,8 +592,7 @@
 
         @pl.when(ysends[way])
         def _():
-            for c in yc[way]:
-                c.wait_send()
+            yall[way].wait_send()
     for c in (*awhole, bwhole):
         c.wait_send()
     mark(None)
@@ -602,7 +610,7 @@
     dz = jnp.concatenate([dz_hi, dz_hi, dz_lo], axis=0)
     ends = closure(CX, CX * N_GX)
     gray = np.arange(BINS) // 8 * 8
-    gray = (gray ^ (gray >> 1) & 56) + ((n := np.arange(BINS) % 8) ^ (n >> 1))
+    gray = (gray ^ (gray >> 1) & 56) + np.arange(BINS) % 8
     common = gray[:, None] & np.arange(BINS)[None, :]
     parity = sum((common >> k) & 1 for k in range(6)) % 2
     had = np.kron(np.eye(2), (1.0 - 2.0 * parity) / BINS).astype(np.float32)
@@ -643,7 +651,7 @@
             vm((N_GX - 1, 2, 128), F32),
             pltpu.SMEM((4, 128), F32),
             pltpu.SMEM((1, FACES_DEV), jnp.int32),
-            dma((5, 2)), dma((10,)), dma((2, 3)), dma((2, 3)), dma((2, 3)), dma((2, 3)),
+            dma((5, 2)), dma((10,)), dma((2, 3)), dma((2, 3)), dma((2,)), dma((2,)),
             dma((2,)), dma((2,)), dma(()), dma(()), pltpu.SemaphoreType.REGULAR((6,)),
         ],
         compiler_params=pltpu.CompilerParams(

time: 35.8 us -> 35.5 us (level)
  no operation moved by 1% of the time
where the time goes in v5:
time: 35.5 us; the launch traced here: 35.1 us
  Pallas kernels  34.4 us (97%)
  between operations  0.64 us (2%)
    pallas_call x1, Pallas kernels, per_device(): pl.pallas_call(functools.partial(kernel, ends), out_shape=(vm((4, CX, CY,...  31.7 us
    pallas_call x1, Pallas kernels, per_device(): pl.pallas_call(write_out, out_shape=(jax.ShapeDtypeStruct((4, CX, CY, NZ)...  2.74 us

profile of v5, /device:TPU:0, one launch (start us, length us, event | category | flops | bytes accessed | tf_op | source)
XLA Modules:
  0.0 35.1 jit_solution(1866547622809604064)
XLA Ops:
  0.6 31.7 %shard_map.122 = (f32[4,32,48,256]{3,2,1,0:T(8,128)S(1)}, f32[4,64]{1,0:T(4,128)S(1)}) custom-call(f32[4,32,48,256]{3,2,1,0:T(8,128)} %state.1, f32[32,48,256]{2,1,0:T(8,128)} %mean.1, s32[1,192]{1,0:T(1,128)} %bitcast.1, f32[3,192]{1,0:T(4,128)} %normal.1, f32[3,192]{1,0:T(4,128)} %pos.1, f32[3,512]{1,0:T(4,128)} %obs.1, s32[192,512]{1,0:T(8,128)} %tbin.1, ...), custom_call_target="tpu_custom_call" | custom-call | tf_op jit(solution)/shard_map/pallas_call | solution.py:620
  32.3 2.7 %shard_map.123 = (f32[4,32,48,256]{3,2,1,0:T(8,128)}, f32[4,64]{1,0:T(4,128)}) custom-call(f32[4,32,48,256]{3,2,1,0:T(8,128)S(1)} %get-tuple-element.4.nxt_ref, f32[4,64]{1,0:T(4,128)S(1)} %get-tuple-element.5.sig_ref), custom_call_target="tpu_custom_call" | custom-call | tf_op jit(solution)/shard_map/pallas_call | solution.py:673

commit v6 on v5

--- a/solution.py
+++ b/solution.py
@@ -310,10 +310,21 @@
             tell(near_sem.at[1], "yz", 2)
             tell(near_sem.at[2], "gx", 2)
         jobs += 2 * per_half
+        even = lax.rem(yz, 2) == 0
         for way in range(2):
-            @pl.when(sends[way])
-            def _():
-                sums[way][f].start()
+            if f in (2, 1, 4):
+                @pl.when(sends[way])
+                def _():
+                    sums[way][f].start()
+            else:
+                @pl.when(jnp.logical_and(sends[way], even))
+                def _():
+                    sums[way][f].start()
+            if f == 2:
+                @pl.when(jnp.logical_and(sends[way], jnp.logical_not(even)))
+                def _():
+                    for k in (0, 3):
+                        sums[way][k].start()
 
     mark("ends")
     for way, there in ((0, jnp.logical_not(has_left)), (1, jnp.logical_not(has_right))):
@@ -376,8 +387,8 @@
     fld_rows = fld.reshape(5, CX * 2 * 64, 128)
 
     def gather(n, _):
-        for k in range(8):
-            j = n * 8 + k
+        for k in range(16):
+            j = n * 16 + k
             cell = cell_s[0, j]
             line = jnp.maximum(lax.shift_right_logical(cell, 8) - corner, 0)
             x = lax.shift_right_logical(lax.shift_right_logical(line, 7) * 86, 8)
@@ -388,7 +399,7 @@
                 stg[q, pl.ds(j, 1), :] = fld_rows[f, pl.ds(row + 8, 1), :]
         return 0
 
-    lax.fori_loop(0, FACES_DEV // 8, gather, 0)
+    lax.fori_loop(0, FACES_DEV // 16, gather, 0)
 
     told(near_sem.at[1], ("yz", 2))
     tell(near_sem.at[3], "yz", 4)

time: 35.5 us -> 35.1 us (0.989)
  no operation moved by 1% of the time
where the time goes in v6:
time: 35.1 us; the launch traced here: 34.7 us
  Pallas kernels  34.1 us (97%)
  between operations  0.64 us (2%)
    pallas_call x1, Pallas kernels, per_device(): pl.pallas_call(functools.partial(kernel, ends), out_shape=(vm((4, CX, CY,...  31.4 us
    pallas_call x1, Pallas kernels, per_device(): pl.pallas_call(write_out, out_shape=(jax.ShapeDtypeStruct((4, CX, CY, NZ)...  2.74 us

profile of v6, /device:TPU:0, one launch (start us, length us, event | category | flops | bytes accessed | tf_op | source)
XLA Modules:
  0.0 34.7 jit_solution(14283989330501976576)
XLA Ops:
  0.6 31.4 %shard_map.122 = (f32[4,32,48,256]{3,2,1,0:T(8,128)S(1)}, f32[4,64]{1,0:T(4,128)S(1)}) custom-call(f32[4,32,48,256]{3,2,1,0:T(8,128)} %state.1, f32[32,48,256]{2,1,0:T(8,128)} %mean.1, s32[1,192]{1,0:T(1,128)} %bitcast.1, f32[3,192]{1,0:T(4,128)} %normal.1, f32[3,192]{1,0:T(4,128)} %pos.1, f32[3,512]{1,0:T(4,128)} %obs.1, s32[192,512]{1,0:T(8,128)} %tbin.1, ...), custom_call_target="tpu_custom_call" | custom-call | tf_op jit(solution)/shard_map/pallas_call | solution.py:631
  32.0 2.7 %shard_map.123 = (f32[4,32,48,256]{3,2,1,0:T(8,128)}, f32[4,64]{1,0:T(4,128)}) custom-call(f32[4,32,48,256]{3,2,1,0:T(8,128)S(1)} %get-tuple-element.4.nxt_ref, f32[4,64]{1,0:T(4,128)S(1)} %get-tuple-element.5.sig_ref), custom_call_target="tpu_custom_call" | custom-call | tf_op jit(solution)/shard_map/pallas_call | solution.py:684

commit v7 on v6

--- a/solution.py
+++ b/solution.py
@@ -326,6 +326,8 @@
                     for k in (0, 3):
                         sums[way][k].start()
 
+    told(near_sem.at[1], ("yz", 2))
+    tell(near_sem.at[3], "yz", 4)
     mark("ends")
     for way, there in ((0, jnp.logical_not(has_left)), (1, jnp.logical_not(has_right))):
         @pl.when(there)
@@ -401,8 +403,6 @@
 
     lax.fori_loop(0, FACES_DEV // 16, gather, 0)
 
-    told(near_sem.at[1], ("yz", 2))
-    tell(near_sem.at[3], "yz", 4)
     told(near_sem.at[2], ("gx", 2))
     tell(near_sem.at[4], "gx", 4)
     mark("picks")
@@ -471,9 +471,13 @@
     def patterns(n, _):
         t = n // 8
         block = n - 8 * t
-        lanes = pl.ds(pl.multiple_of(128 * t, 128), 128)
         after = block + 1
-        bit = jnp.where(after % 2 == 1, 3, jnp.where(after % 4 == 2, 4, 5))
+        if isinstance(n, int):
+            lanes, store = pl.ds(128 * t, 128), 64 * block
+            bit = 3 if after % 2 == 1 else (4 if after % 4 == 2 else 5)
+        else:
+            lanes, store = pl.ds(pl.multiple_of(128 * t, 128), 128), pl.multiple_of(64 * block, 8)
+            bit = jnp.where(after % 2 == 1, 3, jnp.where(after % 4 == 2, 4, 5))
         acc = [jnp.zeros((8, 128), F32)] * 8
         for g in range(FACES_DEV // 8):
             rows = pl.ds(8 * g, 8)
@@ -485,7 +489,7 @@
                 parts += [part * sign for part in parts]
             acc = [a + part for a, part in zip(acc, parts)]
         for k in range(8):
-            binned[t, pl.ds(pl.multiple_of(64 * block, 8) + 8 * k, 8), :] = acc[k]
+            binned[t, pl.ds(store + 8 * k, 8), :] = acc[k]
         return 0
 
     def folded(t):
@@ -516,11 +520,7 @@
     awhole = [whole(recv_a.at[half], as_sem.at[half], ar_sem.at[half], high) for half in range(2)]
     bwhole = whole(recv_b, bs_sem, br_sem, right)
 
-    told(near_sem.at[3], ("yz", 4))
-    for half in range(2):
-        mark(f"bins{half}")
-        lax.fori_loop(16 * half, 16 * half + 16, patterns, 0, unroll=4)
-        mark(f"pack{half}")
+    def pack(half):
         had = had_v[...]
         both = jnp.concatenate([folded(2 * half), folded(2 * half + 1)], axis=0).T
         hi = both.astype(BF16)
@@ -532,11 +532,26 @@
             + jnp.dot(mid, had, preferred_element_type=F32)
             + jnp.dot(lo, had, preferred_element_type=F32)
         )
+
+    def send_half(half):
         for k in (4, 3, 5, 2, 6, 1, 7):
             acopy(half, k).start()
-        if half == 0:
-            told(near_sem.at[4], ("gx", 4))
-            tell(near_sem.at[5], "gx", 8)
+
+    mark("bins0")
+    lax.fori_loop(0, 16, patterns, 0, unroll=4)
+    mark("pack0")
+    pack(0)
+    for n in range(16, 20):
+        patterns(n, 0)
+    told(near_sem.at[3], ("yz", 4))
+    send_half(0)
+    told(near_sem.at[4], ("gx", 4))
+    tell(near_sem.at[5], "gx", 8)
+    mark("bins1")
+    lax.fori_loop(20, 32, patterns, 0, unroll=4)
+    mark("pack1")
+    pack(1)
+    send_half(1)
 
     mark("finish_a")
     def finish(x, _):

time: 35.1 us -> 35 us (level)
  no operation moved by 1% of the time
where the time goes in v7:
time: 35 us; the launch traced here: 34.6 us
  Pallas kernels  34 us (97%)
  between operations  0.64 us (2%)
    pallas_call x1, Pallas kernels, per_device(): pl.pallas_call(functools.partial(kernel, ends), out_shape=(vm((4, CX, CY,...  31.2 us
    pallas_call x1, Pallas kernels, per_device(): pl.pallas_call(write_out, out_shape=(jax.ShapeDtypeStruct((4, CX, CY, NZ)...  2.74 us

profile of v7, /device:TPU:0, one launch (start us, length us, event | category | flops | bytes accessed | tf_op | source)
XLA Modules:
  0.0 34.6 jit_solution(16797982173883430067)
XLA Ops:
  0.6 31.2 %shard_map.122 = (f32[4,32,48,256]{3,2,1,0:T(8,128)S(1)}, f32[4,64]{1,0:T(4,128)S(1)}) custom-call(f32[4,32,48,256]{3,2,1,0:T(8,128)} %state.1, f32[32,48,256]{2,1,0:T(8,128)} %mean.1, s32[1,192]{1,0:T(1,128)} %bitcast.1, f32[3,192]{1,0:T(4,128)} %normal.1, f32[3,192]{1,0:T(4,128)} %pos.1, f32[3,512]{1,0:T(4,128)} %obs.1, s32[192,512]{1,0:T(8,128)} %tbin.1, ...), custom_call_target="tpu_custom_call" | custom-call | tf_op jit(solution)/shard_map/pallas_call | solution.py:646
  31.9 2.7 %shard_map.123 = (f32[4,32,48,256]{3,2,1,0:T(8,128)}, f32[4,64]{1,0:T(4,128)}) custom-call(f32[4,32,48,256]{3,2,1,0:T(8,128)S(1)} %get-tuple-element.4.nxt_ref, f32[4,64]{1,0:T(4,128)S(1)} %get-tuple-element.5.sig_ref), custom_call_target="tpu_custom_call" | custom-call | tf_op jit(solution)/shard_map/pallas_call | solution.py:699

commit v8 on v7

--- a/solution.py
+++ b/solution.py
@@ -126,10 +126,10 @@
         src = mean if f == 4 else state.at[f]
         for t in range(2):
             c = pltpu.make_async_copy(
-                src.at[:, :, pl.ds(128 * t, 128)], fld.at[f, :, t, pl.ds(8, CY), :], ld_sem.at[f, t]
+                src.at[:, :, pl.ds(128 * t, 128)], fld.at[f, :, t, pl.ds(8, CY), :], ld_sem.at[f]
             )
             c.start()
-            loads[f, t] = c
+        loads[f] = pltpu.make_async_copy(src, zed.at[0], ld_sem.at[f])
     mark("barrier_wait")
     told(barrier, ("gx", 1), ("yz", 1))
 
@@ -185,8 +185,7 @@
     ygets = (has_low, has_high)
 
     def send_y(f):
-        loads[f, 0].wait()
-        loads[f, 1].wait()
+        loads[f].wait()
         for way in range(2):
             @pl.when(ysends[way])
             def _():
@@ -277,8 +276,7 @@
     jobs = 0
     for f, per_half in zip((0, 3, 2, 1, 4), (1, 1, 1, 0, 0)):
         if f not in (0, 2, 4):
-            loads[f, 0].wait()
-            loads[f, 1].wait()
+            loads[f].wait()
 
         def sweep(t, _, f=f, per_half=per_half, jobs=jobs):
             zero = jnp.zeros((CY, 128), F32)
@@ -677,7 +675,7 @@
             vm((N_GX - 1, 2, 128), F32),
             pltpu.SMEM((4, 128), F32),
             pltpu.SMEM((1, FACES_DEV), jnp.int32),
-            dma((5, 2)), dma((10,)), dma((2, 3)), dma((2, 3)), dma((2,)), dma((2,)),
+            dma((5,)), dma((10,)), dma((2, 3)), dma((2, 3)), dma((2,)), dma((2,)),
             dma((2,)), dma((2,)), dma(()), dma(()), pltpu.SemaphoreType.REGULAR((6,)),
         ],
         compiler_params=pltpu.CompilerParams(
@@ -689,12 +687,12 @@
     )
 
     def write_out(nxt_ref, sig_ref, nxt_out, sig_out, sem):
-        copies = [pltpu.make_async_copy(sig_ref, sig_out, sem.at[4])]
-        copies += [pltpu.make_async_copy(nxt_ref.at[k], nxt_out.at[k], sem.at[k]) for k in range(4)]
+        copies = [pltpu.make_async_copy(sig_ref, sig_out, sem.at[1])]
+        copies += [pltpu.make_async_copy(nxt_ref.at[k], nxt_out.at[k], sem.at[0]) for k in range(4)]
         for c in copies:
             c.start()
-        for c in copies:
-            c.wait()
+        copies[0].wait()
+        pltpu.make_async_copy(nxt_ref, nxt_out, sem.at[0]).wait()
 
     return pl.pallas_call(
         write_out,
@@ -704,7 +702,7 @@
         ),
         in_specs=[pl.BlockSpec(memory_space=pltpu.VMEM)] * 2,
         out_specs=(anywhere, anywhere),
-        scratch_shapes=[dma((5,))],
+        scratch_shapes=[dma((2,))],
         compiler_params=pltpu.CompilerParams(vmem_limit_bytes=2**20),
     )(pltpu.with_memory_space_constraint(nxt, pltpu.VMEM), pltpu.with_memory_space_constraint(sig, pltpu.VMEM))
 

time: 35 us -> 35 us (level)
  no operation moved by 1% of the time
where the time goes in v8:
time: 35 us; the launch traced here: 34.6 us
  Pallas kernels  33.9 us (97%)
  between operations  0.64 us (2%)
    pallas_call x1, Pallas kernels, per_device(): pl.pallas_call(functools.partial(kernel, ends), out_shape=(vm((4, CX, CY,...  31.2 us
    pallas_call x1, Pallas kernels, per_device(): pl.pallas_call(write_out, out_shape=(jax.ShapeDtypeStruct((4, CX, CY, NZ)...  2.72 us

profile of v8, /device:TPU:0, one launch (start us, length us, event | category | flops | bytes accessed | tf_op | source)
XLA Modules:
  0.0 34.6 jit_solution(12169692118199211563)
XLA Ops:
  0.6 31.2 %shard_map.122 = (f32[4,32,48,256]{3,2,1,0:T(8,128)S(1)}, f32[4,64]{1,0:T(4,128)S(1)}) custom-call(f32[4,32,48,256]{3,2,1,0:T(8,128)} %state.1, f32[32,48,256]{2,1,0:T(8,128)} %mean.1, s32[1,192]{1,0:T(1,128)} %bitcast.1, f32[3,192]{1,0:T(4,128)} %normal.1, f32[3,192]{1,0:T(4,128)} %pos.1, f32[3,512]{1,0:T(4,128)} %obs.1, s32[192,512]{1,0:T(8,128)} %tbin.1, ...), custom_call_target="tpu_custom_call" | custom-call | tf_op jit(solution)/shard_map/pallas_call | solution.py:644
  31.9 2.7 %shard_map.123 = (f32[4,32,48,256]{3,2,1,0:T(8,128)}, f32[4,64]{1,0:T(4,128)}) custom-call(f32[4,32,48,256]{3,2,1,0:T(8,128)S(1)} %get-tuple-element.4.nxt_ref, f32[4,64]{1,0:T(4,128)S(1)} %get-tuple-element.5.sig_ref), custom_call_target="tpu_custom_call" | custom-call | tf_op jit(solution)/shard_map/pallas_call | solution.py:697
